TPU v7x, 128 devices: a whole 4x4x4 slice. The times are simulated.
128 devices in a mesh: seq: 16 (over z, y), ch: 8 (over x, core).
Axes of the slice: x: 4, y: 4, z: 4, core: 2. Of those that a mesh axis runs over, the one named last changes fastest.
Arguments:
- signal: float32 [1, 65536, 1024], P(None, 'seq', 'ch'), may hold values from -6 to 6
- spectrum: float32 [2, 256, 256, 1024], P(None, 'seq', None, 'ch'), may hold values from -6 to 6
- channel_mode: int32 [1024], P('ch'), may hold values 0 or 1
- skip_gain: float32 [1024], P('ch'), may hold values from -4 to 4
- out_weight: bfloat16 [1024, 1024], P('ch'), may hold values from -0.1875 to 0.1875
Outputs:
- projected: float32 [1, 65536, 1024], P(None, 'seq', 'ch')
Inputs may be any that keep to these rules, and one draw needn't show every extreme that they name: `channel_mode`: 1 marks a channel whose 65536 positions are one sequence, 0 a channel whose positions form a 256 x 256 image.
All inputs are finite; a program needn't handle non-finite values. No bound on the sum of `channel_mode` on one device may be relied on, other than what follows from the above.
Results may differ from a plain program's by a relative error of at most 0.017.
Values may be sent and summed in bfloat16 or wider, within the bound.
A program may use at most 128 MiB of HBM per device.

v0:
```python
import math

import jax
import jax.numpy as jnp
from jax import lax
from jax.sharding import Mesh
from jax.sharding import PartitionSpec as P

ROWS = 256
COLUMNS = 256
LENGTH = 65536
CH = ("ch_0", "ch_1")


def cut_along(value, dim, devices):
    lengths = value.shape
    parts = value.reshape(*lengths[:dim], devices, lengths[dim] // devices, *lengths[dim + 1 :])
    return jnp.moveaxis(parts, dim, 0)


def joined_along(parts, dim):
    lengths = list(parts.shape[1:])
    lengths[dim] *= parts.shape[0]
    return jnp.moveaxis(parts, 0, dim).reshape(lengths)


def moved_by_axis(parts, axes, order):
    lengths = [lax.axis_size(a) for a in axes]
    parts = parts.reshape(*lengths, *parts.shape[1:])
    for k in order:
        parts = lax.all_to_all(parts, axes[k], split_axis=k, concat_axis=k, tiled=True)
    return parts.reshape(-1, *parts.shape[len(axes) :])


def exchange_by_axis(value, axes, order, split_dim, concat_dim):
    parts = cut_along(value, split_dim, lax.axis_size(axes))
    return joined_along(moved_by_axis(parts, axes, order), concat_dim)


def contract(pattern, operand, matrix):
    return jnp.einsum(pattern, operand, matrix, preferred_element_type=jnp.float32)


def phase_table(row_index, col_index, period):
    product = row_index[:, None] * col_index[None, :] % period
    angles = product.astype(jnp.float32) * (2.0 * math.pi / period)
    return (jnp.cos(angles), jnp.sin(angles))


def square_table(length):
    counter = jnp.arange(length, dtype=jnp.int32)
    return phase_table(counter, counter, length)


def transform_real(pattern, operand, cosine_table, sine_table):
    return (contract(pattern, operand, cosine_table), -contract(pattern, operand, sine_table))


def transform_complex(pattern, real_part, imag_part, cosine_table, sine_table, orient):
    real_out = contract(pattern, real_part, cosine_table) - orient * contract(
        pattern, imag_part, sine_table
    )
    imag_out = orient * contract(pattern, real_part, sine_table) + contract(
        pattern, imag_part, cosine_table
    )
    return (real_out, imag_out)


def inverse_real(pattern, real_part, imag_part, cosine_table, sine_table, factor):
    return (
        contract(pattern, real_part, cosine_table) - contract(pattern, imag_part, sine_table)
    ) * factor


def rotate(real_part, imag_part, cosine_table, sine_table, orient):
    real_out = real_part * cosine_table - orient * imag_part * sine_table
    imag_out = orient * real_part * sine_table + imag_part * cosine_table
    return (real_out, imag_out)


def filter_product(real_part, imag_part, filter_real, filter_imag):
    return (
        real_part * filter_real - imag_part * filter_imag,
        real_part * filter_imag + imag_part * filter_real,
    )


def channel_plan(signal, spectrum, channel_mode):
    groups = lax.axis_size("seq")
    position = lax.axis_index("seq")
    batches, local_len, owned = signal.shape
    rows_local = ROWS // groups
    shared = owned // groups
    tiled = signal.reshape(batches, rows_local, COLUMNS, owned)
    gathered, filters = (
        lax.all_to_all(
            tiled.astype(jnp.bfloat16), "seq", split_axis=3, concat_axis=1, tiled=True
        ).astype(tiled.dtype),
        lax.all_to_all(
            spectrum.astype(jnp.bfloat16), "seq", split_axis=3, concat_axis=1, tiled=True
        ).astype(spectrum.dtype),
    )
    own_modes = lax.dynamic_slice_in_dim(channel_mode, position * shared, shared)
    selector = (own_modes == 1)[None, :, None, None]
    images = jnp.transpose(gathered, (0, 3, 1, 2))
    filters_first = jnp.transpose(filters, (0, 3, 1, 2))
    row_cos, row_sin = square_table(ROWS)
    col_cos, col_sin = square_table(COLUMNS)
    twist_cos, twist_sin = phase_table(
        jnp.arange(ROWS, dtype=jnp.int32), jnp.arange(COLUMNS, dtype=jnp.int32), LENGTH
    )
    chosen_cos = jnp.where(selector, twist_cos[None, None], 1.0)
    chosen_sin = jnp.where(selector, twist_sin[None, None], 0.0)
    real_part, imag_part = transform_real("xmab,ad->xmdb", images, row_cos, row_sin)
    real_part, imag_part = rotate(real_part, imag_part, chosen_cos, chosen_sin, -1.0)
    real_part, imag_part = transform_complex(
        "xmdb,bc->xmdc", real_part, imag_part, col_cos, col_sin, -1.0
    )
    real_part, imag_part = filter_product(
        real_part, imag_part, filters_first[0][None], filters_first[1][None]
    )
    real_part, imag_part = transform_complex(
        "xmdc,cb->xmdb", real_part, imag_part, col_cos, col_sin, 1.0
    )
    real_part, imag_part = rotate(real_part, imag_part, chosen_cos, chosen_sin, 1.0)
    convolved = inverse_real("xmdb,da->xmab", real_part, imag_part, row_cos, row_sin, 1.0 / LENGTH)
    convolved = jnp.transpose(convolved, (0, 2, 3, 1))
    restored = lax.all_to_all(
        convolved.astype(jnp.bfloat16), "seq", split_axis=1, concat_axis=3, tiled=True
    ).astype(convolved.dtype)
    return restored.reshape(batches, local_len, owned)


def per_device(signal, spectrum, channel_mode, skip_gain, out_weight):
    convolved = channel_plan(signal, spectrum, channel_mode)
    hidden = (convolved + skip_gain[None, None, :] * signal).astype(jnp.bfloat16)
    block_rows = out_weight.shape[0]
    columns = exchange_by_axis(out_weight, CH, (1, 0), 1, 0)
    arrived = lax.all_gather(hidden, CH, axis=2, tiled=True)
    number = arrived.shape[2] // block_rows
    blocks = arrived.reshape(arrived.shape[0], arrived.shape[1], number, block_rows)
    weights = columns
    weights = weights.reshape(number, block_rows, columns.shape[1])
    pieces = jnp.einsum("xtkc,kcj->xtkj", blocks, weights, preferred_element_type=jnp.float32)
    pieces = lax.optimization_barrier(pieces.astype(jnp.bfloat16)).astype(jnp.float32)
    return jnp.sum(pieces, axis=2)


def solution(mesh):
    torus = Mesh(mesh.devices.reshape(mesh.shape["seq"], 4, 2), ("seq", "ch_0", "ch_1"))
    in_specs = (P(None, "seq", CH), P(None, "seq", None, CH), P(CH), P(CH), P(CH, None))
    out_specs = P(None, "seq", CH)
    return jax.shard_map(
        per_device, mesh=torus, in_specs=in_specs, out_specs=out_specs, check_vma=False
    )
```

profile of v0, /device:TPU:0, one launch (start us, length us, event | category | flops | bytes accessed | tf_op | source)
XLA Modules:
  0.0 187.2 jit_solution(17182558534088516674)
XLA Ops:
  6.5 1.7 convert_element_type.119
  8.2 1.7 copy.133
  9.9 8.2 %all-to-all-start = ((bf16[1,16,256,128]{2,1,0,3:T(8,128)(2,1)}), bf16[1,16,256,128]{2,1,0,3:T(8,128)(2,1)S(1)}, u32[]{:S(2)}, u32[]{:S(2)}) async-start(bf16[1,16,256,128]{2,1,0,3:T(8,128)(2,1)} %copy.133), calls=%async_computation | async-start | bytes 2097152 | tf_op jit(solution)/shard_map/all_to_all | solution.py:96
  20.3 5.1 %copy.140 = bf16[2,16,256,128]{2,1,0,3:T(8,128)(2,1)} copy(f32[2,16,256,128]{3,2,1,0:T(8,128)} %param.6) | data formatting | bytes 6291456 | tf_op args[1]
  25.4 10.4 %all-to-all-done = bf16[1,16,256,128]{2,1,0,3:T(8,128)(2,1)S(1)} async-done(((bf16[1,16,256,128]{2,1,0,3:T(8,128)(2,1)}), bf16[1,16,256,128]{2,1,0,3:T(8,128)(2,1)S(1)}, u32[]{:S(2)}, u32[]{:S(2)}) %all-to-all-start) | async-done | bytes 1048608 | tf_op jit(solution)/shard_map/all_to_all | solution.py:96
  35.8 4.6 %all-to-all-start.1 = ((bf16[2,16,256,128]{2,1,0,3:T(8,128)(2,1)}), bf16[2,16,256,128]{2,1,0,3:T(8,128)(2,1)}, u32[]{:S(2)}, u32[]{:S(2)}) async-start(bf16[2,16,256,128]{2,1,0,3:T(8,128)(2,1)} %copy.140), calls=%async_computation.1 | async-start | bytes 4194304 | tf_op jit(solution)/shard_map/all_to_all | solution.py:99
  42.7 1.4 fusion.51
  44.1 1.6 fusion.56
  45.7 2.9 %fusion.47 = f32[8,256,256]{2,1,0:T(8,128)} fusion(f32[256,8,256]{2,0,1:T(8,128)S(1)} %fusion.59, f32[256,8,256]{2,0,1:T(8,128)S(1)} %fusion.51, f32[256,256]{1,0:T(8,128)S(1)} %copy.137, f32[256,256]{1,0:T(8,128)S(1)} %copy.136, pred[8]{0:T(512)(128)(4,1)S(1)} %dynamic-slice_compare_fusion), kind=kOutput, calls=%fused_computation.65 | convolution fusion | flops 273022976 | bytes 6815752 | tf_op jit(solution)/shard_map/xmdb,bc->xmdc/dot_general | solution.py:41
  48.6 3.1 %multiply_subtract_fusion = f32[8,256,256]{2,1,0:T(8,128)} fusion(f32[8,256,256]{2,1,0:T(8,128)S(1)} %fusion.56, f32[256,8,256]{2,0,1:T(8,128)S(1)} %fusion.59, f32[256,8,256]{2,0,1:T(8,128)S(1)} %fusion.51, f32[256,256]{1,0:T(8,128)S(1)} %copy.137, f32[256,256]{1,0:T(8,128)S(1)} %copy.136, pred[8]{0:T(512)(128)(4,1)S(1)} %dynamic-slice_compare_fusion), kind=kOutput, calls=%fused_computation.39 | convolution fusion | flops 274071552 | bytes 8912904 | tf_op jit(solution)/shard_map/xmdb,bc->xmdc/dot_general | solution.py:41
  51.8 17.2 %all-to-all-done.1 = bf16[2,16,256,128]{2,1,0,3:T(8,128)(2,1)} async-done(((bf16[2,16,256,128]{2,1,0,3:T(8,128)(2,1)}), bf16[2,16,256,128]{2,1,0,3:T(8,128)(2,1)}, u32[]{:S(2)}, u32[]{:S(2)}) %all-to-all-start.1) | async-done | bytes 2097184 | tf_op jit(solution)/shard_map/all_to_all | solution.py:99
  68.9 2.8 %convert_bitcast_fusion.1 = f32[2,16,16,256,8]{3,4,1,2,0:T(8,128)S(1)} fusion(bf16[2,16,256,128]{2,1,0,3:T(8,128)(2,1)} %all-to-all-done.1), kind=kLoop, calls=%fused_computation.2 | loop fusion | flops 1048576 | bytes 6291456 | tf_op jit(solution)/shard_map/transpose | solution.py:106
  71.8 2.7 %copy.142 = f32[2,16,16,256,8]{3,2,1,4,0:T(8,128)S(1)} copy(f32[2,16,16,256,8]{3,4,1,2,0:T(8,128)S(1)} %convert_bitcast_fusion.1) | data formatting | bytes 8388608 | tf_op jit(solution)/shard_map/transpose | solution.py:106
  74.6 2.1 %fusion.18 = (bf16[1,8,256,256]{3,2,1,0:T(8,128)(2,1)S(1)}, bf16[1,8,256,256]{3,2,1,0:T(8,128)(2,1)S(1)}) fusion(f32[8,256,256]{2,1,0:T(8,128)S(1)} %copy-done.2, f32[2,8,256,256]{3,2,1,0:T(8,128)S(1)} %bitcast.152, f32[256,8,256]{2,0,1:T(8,128)S(1)} %fusion.59, f32[256,8,256]{2,0,1:T(8,128)S(1)} %copy-done.1, f32[256,256]{1,0:T(8,128)S(1)} %copy.137, ...), kind=kOutput, calls=%fused_computation.29 | convolution fusion | flops 278265856 | bytes 15204360 | tf_op jit(solution)/shard_map/xmdb,bc->xmdc/dot_general | solution.py:41
  76.7 1.4 fusion.12
  78.1 1.4 fusion.10
  79.5 1.4 fusion.20
  80.9 1.4 fusion.23
  82.3 1.7 fusion.5
  84.0 1.8 fusion.28
  85.9 1.6 copy.151
  87.4 3.7 %all-to-all-start.2 = ((bf16[1,256,256,8]{2,3,0,1:T(8,128)(2,1)}), bf16[1,256,256,8]{2,3,0,1:T(8,128)(2,1)S(1)}, u32[]{:S(2)}, u32[]{:S(2)}) async-start(bf16[1,256,256,8]{2,3,0,1:T(8,128)(2,1)} %copy.151), calls=%async_computation.2 | async-start | bytes 2097152 | tf_op jit(solution)/shard_map/all_to_all | solution.py:128
  91.2 2.1 %copy.153 = f32[1,4096,128]{1,2,0:T(8,128)} copy(f32[1,4096,128]{2,1,0:T(8,128)S(1)} %copy-done.4) | data formatting | bytes 4194304 | tf_op args[0]
  93.3 14.8 %all-to-all-done.2 = bf16[1,256,256,8]{2,3,0,1:T(8,128)(2,1)S(1)} async-done(((bf16[1,256,256,8]{2,3,0,1:T(8,128)(2,1)}), bf16[1,256,256,8]{2,3,0,1:T(8,128)(2,1)S(1)}, u32[]{:S(2)}, u32[]{:S(2)}) %all-to-all-start.2) | async-done | bytes 1048608 | tf_op jit(solution)/shard_map/all_to_all | solution.py:128
  108.0 1.6 copy.181
  109.7 2.9 %reshape.165 = f32[1,4096,128]{1,2,0:T(8,128)} reshape(f32[1,16,256,16,8]{2,1,4,3,0:T(8,128)} %bitcast.154) | data formatting | bytes 4194304 | tf_op jit(solution)/shard_map/convert_element_type | solution.py:130
  112.6 2.9 %add_convert_fusion = bf16[1,4096,128]{1,2,0:T(8,128)(2,1)} fusion(f32[1,4096,128]{1,2,0:T(8,128)} %reshape.165, f32[1,4096,128]{1,2,0:T(8,128)S(1)} %copy-done.5, f32[128]{0:T(128)S(1)} %copy-done.7), kind=kLoop, calls=%fused_computation.36 | loop fusion | flops 1572864 | bytes 5243392 | tf_op jit(solution)/shard_map/convert_element_type | solution.py:136
  115.9 3.9 %all_to_all.46 = bf16[4,2,128,128]{3,2,0,1:T(8,128)(2,1)S(1)} all-to-all(bf16[4,2,128,128]{3,2,0,1:T(8,128)(2,1)S(1)} %copy.156), channel_id=1, replica_groups=mesh['seq'=16,'ch_0'=4,'ch_1'=2] {'ch_1'}, dimensions={1} | all-to-all | bytes 524288 | tf_op jit(solution)/shard_map/all_to_all | solution.py:31
  119.8 14.6 %all_to_all.47 = bf16[4,2,128,128]{3,2,1,0:T(8,128)(2,1)S(1)} all-to-all(bf16[4,2,128,128]{3,2,1,0:T(8,128)(2,1)S(1)} %copy.157), channel_id=1, replica_groups=mesh['seq'=16,'ch_0'=4,'ch_1'=2] {'ch_0'}, dimensions={0} | all-to-all | bytes 524288 | tf_op jit(solution)/shard_map/all_to_all | solution.py:31
  134.5 30.6 %all-gather.2.cloned.1.call-done = bf16[1,4096,1024]{1,2,0:T(8,128)(2,1)} async-done(((bf16[1,4096,128]{1,2,0:T(8,128)(2,1)}), bf16[1,4096,1024]{1,2,0:T(8,128)(2,1)}) %all-gather.2.cloned.1.call-update) | async-done | bytes 8388624 | tf_op jit(solution)/shard_map/all_gather | solution.py:139
  165.1 9.3 %convert_bitcast_fusion = bf16[1,4096,8,128]{3,1,2,0:T(8,128)(2,1)} fusion(bf16[4096,8,128]{0,2,1:T(8,128)(2,1)} %bitcast.153, bf16[8,128,128]{2,1,0:T(8,128)(2,1)S(1)} %bitcast.158), kind=kOutput, calls=%fused_computation.1 | convolution fusion | flops 1077936128 | bytes 17039360 | tf_op jit(solution)/shard_map/xtkc,kcj->xtkj/dot_general | solution.py:144
  174.3 6.0 %convert_reduce_fusion = f32[4096,128]{1,0:T(8,128)} fusion(bf16[1,4096,8,128]{3,1,2,0:T(8,128)(2,1)} %convert_bitcast_fusion), kind=kLoop, calls=%fused_computation | loop fusion | flops 7864320 | bytes 10485760 | tf_op jit(solution)/shard_map/reduce_sum | solution.py:146
  (31 shorter events, 5.1 us)
Async XLA Ops:
  9.9 25.8 %all-to-all-start = ((bf16[1,16,256,128]{2,1,0,3:T(8,128)(2,1)}), bf16[1,16,256,128]{2,1,0,3:T(8,128)(2,1)S(1)}, u32[]{:S(2)}, u32[]{:S(2)}) async-start(bf16[1,16,256,128]{2,1,0,3:T(8,128)(2,1)} %copy.133), calls=%async_computation | async-start | bytes 2097152 | tf_op jit(solution)/shard_map/all_to_all | solution.py:96
  25.4 15.0 %copy-start.8 = (s32[128]{0:T(128)S(1)}, s32[128]{0:T(128)}, u32[]{:S(2)}) copy-start(s32[128]{0:T(128)} %param.7) | copy-start | bytes 1540
  35.8 33.2 %all-to-all-start.1 = ((bf16[2,16,256,128]{2,1,0,3:T(8,128)(2,1)}), bf16[2,16,256,128]{2,1,0,3:T(8,128)(2,1)}, u32[]{:S(2)}, u32[]{:S(2)}) async-start(bf16[2,16,256,128]{2,1,0,3:T(8,128)(2,1)} %copy.140), calls=%async_computation.1 | async-start | bytes 4194304 | tf_op jit(solution)/shard_map/all_to_all | solution.py:99
  44.1 4.5 %copy-start = (f32[256,8,256]{2,0,1:T(8,128)}, f32[256,8,256]{2,0,1:T(8,128)S(1)}, u32[]{:S(2)}) copy-start(f32[256,8,256]{2,0,1:T(8,128)S(1)} %fusion.51) | copy-start | bytes 6291460
  71.8 2.7 %copy-start.1 = (f32[256,8,256]{2,0,1:T(8,128)S(1)}, f32[256,8,256]{2,0,1:T(8,128)}, u32[]{:S(2)}) copy-start(f32[256,8,256]{2,0,1:T(8,128)} %copy-done) | copy-start | bytes 6291460
  71.8 2.7 %copy-start.2 = (f32[8,256,256]{2,1,0:T(8,128)S(1)}, f32[8,256,256]{2,1,0:T(8,128)}, u32[]{:S(2)}) copy-start(f32[8,256,256]{2,1,0:T(8,128)} %multiply_subtract_fusion) | copy-start | bytes 6291460
  71.8 2.8 %copy-start.3 = (f32[8,256,256]{2,1,0:T(8,128)S(1)}, f32[8,256,256]{2,1,0:T(8,128)}, u32[]{:S(2)}) copy-start(f32[8,256,256]{2,1,0:T(8,128)} %fusion.47) | copy-start | bytes 6291460
  85.9 5.3 %copy-start.4 = (f32[1,4096,128]{2,1,0:T(8,128)S(1)}, f32[1,4096,128]{2,1,0:T(8,128)}, u32[]{:S(2)}) copy-start(f32[1,4096,128]{2,1,0:T(8,128)} %param.5) | copy-start | bytes 6291460
  87.4 20.6 %all-to-all-start.2 = ((bf16[1,256,256,8]{2,3,0,1:T(8,128)(2,1)}), bf16[1,256,256,8]{2,3,0,1:T(8,128)(2,1)S(1)}, u32[]{:S(2)}, u32[]{:S(2)}) async-start(bf16[1,256,256,8]{2,3,0,1:T(8,128)(2,1)} %copy.151), calls=%async_computation.2 | async-start | bytes 2097152 | tf_op jit(solution)/shard_map/all_to_all | solution.py:128
  91.1 74.0 %all-gather.2.cloned.1.call-start = ((), (), s32[]{:S(2)}) async-start(), calls=%async_computation.5 | async-start | bytes 9437184 | tf_op jit(solution)/shard_map/all_gather | solution.py:139
  109.7 2.9 %copy-start.5 = (f32[1,4096,128]{1,2,0:T(8,128)S(1)}, f32[1,4096,128]{1,2,0:T(8,128)}, u32[]{:S(2)}) copy-start(f32[1,4096,128]{1,2,0:T(8,128)} %copy.153) | copy-start | bytes 6291460
  109.7 2.9 %copy-start.7 = (f32[128]{0:T(128)S(1)}, f32[128]{0:T(128)}, u32[]{:S(2)}) copy-start(f32[128]{0:T(128)} %param.8) | copy-start | bytes 1540
  112.6 2.9 %copy-start.6 = (bf16[128,1024]{1,0:T(8,128)(2,1)S(1)}, bf16[128,1024]{1,0:T(8,128)(2,1)}, u32[]{:S(2)}) copy-start(bf16[128,1024]{1,0:T(8,128)(2,1)} %param.9) | copy-start | bytes 786436
Sparse Core Ops, SparseCore 0:
  115.6 49.4 all-gather.1
where the time goes:
time: 189 us; the launch traced here: 187 us
  waiting for transfers between devices  72.9 us (39%)
  matrix products  30.8 us (16%)
  local copies, waits for them, and re-layouts  19.3 us (10%)
  blocking collectives  18.6 us (10%)
  starting transfers between devices  16.5 us (9%)
  other arithmetic  15.5 us (8%)
  between operations  13.6 us (7%)
    all_gather x1, waiting for transfers between devices, per_device(): arrived = lax.all_gather(hidden, CH, axis=2, tiled=True)  30.6 us
    dot_general x12, matrix products, contract(): jnp.einsum(pattern, operand, matrix, preferred_element_type=jnp.float32)  21.5 us
    all_to_all x2, blocking collectives, moved_by_axis(): lax.all_to_all(parts, axes[k], split_axis=k, concat_axis=k, tiled=True)  18.6 us
    all_to_all x1, waiting for transfers between devices, channel_plan(): lax.all_to_all(spectrum.astype(jnp.bfloat16), 'seq', split_axis=3, concat...  17.2 us
    all_to_all x1, waiting for transfers between devices, channel_plan(): lax.all_to_all(convolved.astype(jnp.bfloat16), 'seq', split_axis=1, conca...  14.8 us
    all_to_all x1, waiting for transfers between devices, channel_plan(): lax.all_to_all(tiled.astype(jnp.bfloat16), 'seq', split_axis=3, concat_ax...  10.4 us
    dot_general x1, matrix products, per_device(): jnp.einsum('xtkc,kcj->xtkj', blocks, weights, preferred_element_type=jnp....  9.26 us
    all_to_all x1, starting transfers between devices, channel_plan(): lax.all_to_all(tiled.astype(jnp.bfloat16), 'seq', split_axis=3, concat_ax...  8.16 us
  transfers between devices with their start and end apart: 4, of which 4 were waited for; matrix products, arithmetic and copies ran while one was open for 11% of the time, Pallas kernels for 0%

commit v1 on v0

v1 whole, which is shorter than its diff:
```python
import math

import jax
import jax.numpy as jnp
import numpy as np
from jax import lax
from jax.experimental import pallas as pl
from jax.experimental.pallas import tpu as pltpu
from jax.sharding import PartitionSpec as P

ROWS = 256
COLUMNS = 256
LENGTH = 65536
BF16 = jnp.bfloat16
F32 = jnp.float32
MESH = pl.DeviceIdType.MESH


def tables():
    counter = np.arange(256)
    angle = (counter[:, None] * counter[None, :] % 256) * (2.0 * math.pi / 256)
    c, s = np.cos(angle), np.sin(angle)
    first = np.concatenate([c, -s], 0)
    second = np.block([[c, -s], [s, c]])
    third = np.block([[c, s], [-s, c]])
    last = np.concatenate([c, -s], 1) / LENGTH
    twist = counter[:, None] * counter[None, :] * (2.0 * math.pi / LENGTH)
    twist = np.stack([np.cos(twist), np.sin(twist)])
    scatter = np.zeros((64, 64))
    for m in range(4):
        for a in range(16):
            x, k, a2 = a // 4, a // 2 % 2, a % 2
            scatter[((k * 4 + x) * 2 + a2) * 4 + m, m * 16 + a] = 1
    regroup = np.zeros((256, 256))
    for h in range(2):
        for s in range(16):
            for a2 in range(2):
                for m in range(4):
                    regroup[((h * 16 + s) * 2 + a2) * 4 + m, a2 * 128 + s * 8 + h * 4 + m] = 1
    half = [jnp.asarray(t, BF16) for t in (first, second, third, last, scatter, regroup)]
    return half + [jnp.asarray(twist, F32)]


def flip(v, mask):
    if mask == 0:
        return v
    if mask == 1:
        return v + 1 - 2 * lax.rem(v, 2)
    if mask == 2:
        return lax.rem(v + 2, 4)
    return 3 - v


def dot(a, b):
    return jnp.dot(a, b, preferred_element_type=F32)


def kernel(
    src, w, mode, gain, first, second, third, last, scatter, regroup, twist,
    out,
    zrel, zbuf, yrel, final, spectral, hid, send, bzrel, bzbuf, byrel, bfinal,
    swap, xrel, gathered, rows, wfull, prod, swap2, xrel2,
    a_sems, b_sems, w_sems, c_sems, d_sems,
):
    s = lax.axis_index("seq")
    c = lax.axis_index("ch")
    z, y, x, k = s // 4, lax.rem(s, 4), c // 2, lax.rem(c, 2)
    other = 1 - k

    def zdev(mask):
        return {"seq": flip(z, mask) * 4 + y, "ch": c}

    def ydev(mask):
        return {"seq": z * 4 + flip(y, mask), "ch": c}

    def xdev(mask):
        return {"seq": s, "ch": flip(x, mask) * 2 + k}

    partner = {"seq": s, "ch": x * 2 + other}

    def copy(a, b, ss, rs, dev):
        return pltpu.make_async_remote_copy(a, b, ss, rs, device_id=dev, device_id_type=MESH)

    def recv(ref, sem):
        copy(ref, ref, sem, sem, partner).wait_recv()

    def sent(ref, sem):
        copy(ref, ref, sem, sem, partner).wait_send()

    barrier = pltpu.get_barrier_semaphore()
    for dev in (zdev(1), zdev(3), ydev(1), ydev(3), xdev(1), xdev(3), partner):
        pl.semaphore_signal(barrier, 1, device_id=dev, device_id_type=MESH)
    pl.semaphore_wait(barrier, 7)

    class Plane:
        def __init__(self, src, zrel, zbuf, yrel, final, sems):
            self.src, self.zrel, self.zbuf, self.yrel, self.final = src, zrel, zbuf, yrel, final
            self.sz, self.sy, self.rzrel, self.rfin, self.rz, self.ryrel = sems

        def zsend(self, q):
            def part(mask):
                return self.src.at[q, pl.ds(4 * flip(z, mask), 4)]

            copy(part(2), self.zrel.at[q], self.sz.at[q], self.rzrel.at[q], zdev(1)).start()
            copy(part(3), self.zbuf.at[q, 2], self.sz.at[q], self.rz.at[q, 2], zdev(3)).start()
            copy(part(1), self.zbuf.at[q, 0], self.sz.at[q], self.rz.at[q, 0], zdev(1)).start()

        def zfwd(self, q):
            recv(self.zrel.at[q], self.rzrel.at[q])
            copy(
                self.zrel.at[q], self.zbuf.at[q, 1], self.sz.at[q], self.rz.at[q, 1], zdev(3)
            ).start()

        def ysend(self, q, mz):
            if mz:
                recv(self.zbuf.at[q, mz - 1], self.rz.at[q, mz - 1])

            def part(mask):
                if mz:
                    return self.zbuf.at[q, mz - 1, flip(y, mask)]
                return self.src.at[q, z * 4 + flip(y, mask)]

            slot = self.final.at[q, flip(z, mz) * 4 + y]
            copy(part(2), self.yrel.at[q, mz], self.sy.at[q], self.ryrel.at[q, mz], ydev(1)).start()
            copy(part(3), slot, self.sy.at[q], self.rfin.at[q], ydev(3)).start()
            copy(part(1), slot, self.sy.at[q], self.rfin.at[q], ydev(1)).start()
            slot[...] = part(0)[...]

        def yfwd(self, q, mz):
            recv(self.yrel.at[q, mz], self.ryrel.at[q, mz])
            slot = self.final.at[q, flip(z, mz) * 4 + flip(y, 1)]
            copy(self.yrel.at[q, mz], slot, self.sy.at[q], self.rfin.at[q], ydev(3)).start()

        def done(self, q):
            recv(self.final.at[q, pl.ds(0, 12)], self.rfin.at[q])

        def drain(self, q):
            sent(self.src.at[q], self.sz.at[q])
            sent(self.src.at[q], self.sy.at[q])

    first_plane = Plane(src, zrel, zbuf, yrel, final, a_sems)
    back = Plane(send, bzrel, bzbuf, byrel, bfinal, b_sems)
    A = first_plane

    def forward(h):
        def step(m, carry):
            image = final[0, :, h, m].reshape(256, 256)
            value = dot(first[...], image)
            re, im = value[:256], value[256:]
            on = mode[4 * h + m] > 0.5
            tc, ts = jnp.where(on, twist[0], 1.0), jnp.where(on, twist[1], 0.0)
            pair = jnp.concatenate([re * tc + im * ts, im * tc - re * ts], 1).astype(BF16)
            spectral[4 * h + m] = dot(pair, second[...])
            return carry

        lax.fori_loop(0, 4, step, 0)

    def inverse(h):
        def step(m, carry):
            value = spectral[4 * h + m]
            re, im = value[:, :256], value[:, 256:]
            fr = final[1 + h, :, 0, m].reshape(256, 256).astype(F32)
            fi = final[1 + h, :, 1, m].reshape(256, 256).astype(F32)
            pair = jnp.concatenate([re * fr - im * fi, re * fi + im * fr], 1).astype(BF16)
            value = dot(pair, third[...])
            re, im = value[:, :256], value[:, 256:]
            on = mode[4 * h + m] > 0.5
            tc, ts = jnp.where(on, twist[0], 1.0), jnp.where(on, twist[1], 0.0)
            pair = jnp.concatenate([re * tc - im * ts, re * ts + im * tc], 0).astype(BF16)
            value = dot(last[...], pair)
            image = final[0, :, h, m].reshape(256, 256).astype(F32)
            value = value + gain[4 * h + m] * image
            hid[m] = value.astype(BF16).reshape(16, 16, 256)
            return carry

        lax.fori_loop(0, 4, step, 0)

        def place(t, carry):
            block = hid[:, t].reshape(64, 256)
            send[h, t] = dot(scatter[...], block).astype(BF16).reshape(2, 4, 8, 256)
            return carry

        lax.fori_loop(0, 16, place, 0)

    A.zsend(0)
    A.ysend(0, 0)
    A.zsend(1)
    A.ysend(1, 0)
    A.ysend(2, 0)

    own = pl.ds(pl.multiple_of(c * 128, 128), 128)

    def wrows(mask):
        return wfull.at[pl.ds(pl.multiple_of((flip(x, mask) * 2 + k) * 128, 128), 128)]

    ws, wx, wp = w_sems
    copy(w, wfull.at[own], ws, wx.at[0], xdev(1)).start()
    copy(w, wfull.at[own], ws, wx.at[2], xdev(3)).start()
    copy(w, wfull.at[own], ws, wp.at[0], partner).start()
    wfull[own] = w[...]

    A.yfwd(0, 0)
    A.zfwd(0)
    A.zsend(2)
    A.ysend(0, 3)
    A.yfwd(1, 0)
    A.yfwd(2, 0)
    recv(wrows(1), wx.at[0])
    copy(wrows(1), wrows(1), ws, wx.at[1], xdev(3)).start()
    copy(wrows(1), wrows(1), ws, wp.at[1], partner).start()
    A.ysend(0, 1)
    A.ysend(1, 3)
    A.yfwd(0, 3)
    A.yfwd(0, 1)
    A.zfwd(1)
    recv(wrows(3), wx.at[2])
    copy(wrows(3), wrows(3), ws, wp.at[3], partner).start()
    A.ysend(0, 2)
    A.yfwd(1, 3)
    A.ysend(1, 1)
    A.yfwd(0, 2)
    recv(wrows(2), wx.at[1])
    copy(wrows(2), wrows(2), ws, wp.at[2], partner).start()
    A.ysend(2, 3)
    A.zfwd(2)
    A.yfwd(1, 1)
    A.done(0)
    forward(0)
    A.ysend(1, 2)
    A.yfwd(2, 3)
    A.yfwd(1, 2)
    forward(1)
    A.ysend(2, 1)
    A.ysend(2, 2)
    A.done(1)
    inverse(0)
    back.zsend(0)
    A.yfwd(2, 1)
    A.yfwd(2, 2)
    back.ysend(0, 0)
    back.yfwd(0, 0)
    back.zfwd(0)
    A.done(2)
    inverse(1)
    back.zsend(1)
    back.ysend(0, 3)
    back.ysend(0, 1)
    back.ysend(1, 0)
    back.yfwd(0, 3)
    back.yfwd(0, 1)
    back.ysend(0, 2)
    back.zfwd(1)
    back.yfwd(1, 0)
    back.yfwd(0, 2)

    es, er, xs, xr, fr = c_sems

    def xsend(h, i):
        kept = k if i == 0 else other

        def part(mask):
            if i == 0:
                return bfinal.at[h, :, k, flip(x, mask)]
            return swap.at[h, :, flip(x, mask)]

        slot = gathered.at[x, kept, h]
        copy(part(2), xrel.at[h, i], xs, xr.at[h, i], xdev(1)).start()
        copy(part(3), slot, xs, fr, xdev(3)).start()
        copy(part(1), slot, xs, fr, xdev(1)).start()
        slot[...] = part(0)[...]

    def xfwd(h, i):
        kept = k if i == 0 else other
        recv(xrel.at[h, i], xr.at[h, i])
        copy(xrel.at[h, i], gathered.at[flip(x, 1), kept, h], xs, fr, xdev(3)).start()

    def exchange(h):
        back.done(h)
        copy(bfinal.at[h, :, other], swap.at[h], es, er.at[h], partner).start()
        xsend(h, 0)

    exchange(0)
    back.ysend(1, 3)
    back.ysend(1, 1)
    recv(swap.at[0], er.at[0])
    xsend(0, 1)
    back.yfwd(1, 3)
    back.yfwd(1, 1)
    back.ysend(1, 2)
    xfwd(0, 0)
    back.yfwd(1, 2)
    xfwd(0, 1)
    exchange(1)
    recv(swap.at[1], er.at[1])
    xsend(1, 1)
    xfwd(1, 0)
    xfwd(1, 1)
    for mask in range(4):
        recv(wfull.at[pl.ds(0, 128)], wp.at[mask])
    recv(gathered.at[pl.ds(0, 3)], fr)

    for i in range(8):
        block = gathered[i // 2, i % 2].reshape(256, 256)
        value = lax.dot_general(
            block, regroup[...], (((0,), (0,)), ((), ())), preferred_element_type=F32
        ).astype(BF16)
        rows[0, :, i * 128 : (i + 1) * 128] = value[:, :128]
        rows[1, :, i * 128 : (i + 1) * 128] = value[:, 128:]

    for i in range(4):
        value = dot(rows[...].reshape(512, 1024), wfull[:, i * 256 : (i + 1) * 256]).astype(BF16)
        prod[0, i] = value[:, :128]
        prod[1, i] = value[:, 128:]

    ds, dr, dxs, dxr, dout = d_sems
    copy(prod.at[other], swap2, ds, dr, partner).start()

    def osend(i):
        kept = k if i == 0 else other

        def part(mask):
            if i == 0:
                return prod.at[k, flip(x, mask)]
            return swap2.at[flip(x, mask)]

        slot = out.at[x * 2 + kept]
        copy(part(2), xrel2.at[i], dxs, dxr.at[i], xdev(1)).start()
        copy(part(3), slot, dxs, dout, xdev(3)).start()
        copy(part(1), slot, dxs, dout, xdev(1)).start()
        slot[...] = part(0)[...]

    def ofwd(i):
        kept = k if i == 0 else other
        recv(xrel2.at[i], dxr.at[i])
        copy(xrel2.at[i], out.at[flip(x, 1) * 2 + kept], dxs, dout, xdev(3)).start()

    osend(0)
    recv(swap2, dr)
    osend(1)
    ofwd(0)
    ofwd(1)
    recv(out.at[pl.ds(0, 6)], dout)

    for q in range(3):
        A.drain(q)
    for h in range(2):
        back.drain(h)
    sent(wfull.at[pl.ds(0, 7 * 128)], ws)
    sent(swap, es)
    sent(gathered, xs)
    sent(swap2, ds)
    sent(out, dxs)


def per_device(signal, spectrum, channel_mode, skip_gain, out_weight):
    s = lax.axis_index("seq")
    pieces = signal.reshape(16, 256, 128).astype(BF16).transpose(2, 0, 1)
    pieces = pieces.reshape(1, 16, 2, 4, 16, 256)
    filters = spectrum.astype(BF16).reshape(2, 16, 256, 16, 2, 4)
    filters = filters.transpose(4, 3, 0, 5, 1, 2)
    source = jnp.concatenate([pieces, filters], 0)
    mode = lax.dynamic_slice_in_dim(channel_mode, s * 8, 8).astype(F32)
    gain = lax.dynamic_slice_in_dim(skip_gain, s * 8, 8)
    unit = (2, 4, 16, 256)
    small = (2, 4, 8, 256)
    dma = pltpu.SemaphoreType.DMA

    def plane(n):
        return (dma((n,)), dma((n,)), dma((n,)), dma((n,)), dma((n, 3)), dma((n, 4)))

    vmem = pl.BlockSpec(memory_space=pltpu.VMEM)
    smem = pl.BlockSpec(memory_space=pltpu.SMEM)
    result = pl.pallas_call(
        kernel,
        out_shape=jax.ShapeDtypeStruct((8, 512, 128), BF16),
        in_specs=[vmem, vmem, smem, smem] + [vmem] * 7,
        out_specs=vmem,
        scratch_shapes=[
            pltpu.VMEM((3, 4) + unit, BF16),
            pltpu.VMEM((3, 3, 4) + unit, BF16),
            pltpu.VMEM((3, 4) + unit, BF16),
            pltpu.VMEM((3, 16) + unit, BF16),
            pltpu.VMEM((8, 256, 512), F32),
            pltpu.VMEM((4, 16, 16, 256), BF16),
            pltpu.VMEM((2, 16) + small, BF16),
            pltpu.VMEM((2, 4) + small, BF16),
            pltpu.VMEM((2, 3, 4) + small, BF16),
            pltpu.VMEM((2, 4) + small, BF16),
            pltpu.VMEM((2, 16) + small, BF16),
            pltpu.VMEM((2, 16, 4, 8, 256), BF16),
            pltpu.VMEM((2, 2, 16, 8, 256), BF16),
            pltpu.VMEM((4, 2, 2, 16, 8, 256), BF16),
            pltpu.VMEM((2, 256, 1024), BF16),
            pltpu.VMEM((1024, 1024), BF16),
            pltpu.VMEM((2, 4, 512, 128), BF16),
            pltpu.VMEM((4, 512, 128), BF16),
            pltpu.VMEM((2, 512, 128), BF16),
            plane(3),
            plane(2),
            (dma, dma((3,)), dma((4,))),
            (dma, dma((2,)), dma, dma((2, 2)), dma),
            (dma, dma, dma, dma((2,)), dma),
        ],
        compiler_params=pltpu.CompilerParams(
            collective_id=0, has_side_effects=True, vmem_limit_bytes=60 << 20
        ),
        name="hyena",
    )(source, out_weight, mode, gain, *tables())
    return result.astype(F32).reshape(1, 4096, 128)


def solution(mesh):
    in_specs = (
        P(None, "seq", "ch"), P(None, "seq", None, "ch"), P("ch"), P("ch"), P("ch", None)
    )
    return jax.shard_map(
        per_device, mesh=mesh, in_specs=in_specs, out_specs=P(None, "seq", "ch"), check_vma=False
    )
```

time: 189 us -> 125 us (0.66)
  Pallas kernels: 0 us -> 108 us
  waiting for transfers between devices: 72.9 us -> 0 us
  matrix products: 30.8 us -> 0 us
  blocking collectives: 18.6 us -> 0 us
  starting transfers between devices: 16.5 us -> 0 us
  between operations: 13.6 us -> 0.03 us
  local copies, waits for them, and re-layouts: 19.3 us -> 9.49 us
  other arithmetic: 15.5 us -> 6.54 us
    pallas_call x0 -> x1, Pallas kernels: none -> 108 us  [per_device(): pl.pallas_call(kernel, out_shape=jax.ShapeDtypeStruct((8, 512, 128), BF16...]
    all_to_all x3 -> x0, waiting for transfers between devices: 42.3 us -> none  [the longest x1 17.2 us: channel_plan(): lax.all_to_all(spectrum.astype(jnp.bfloat16), 'seq', split_axis=3, concat...]
    dot_general x13 -> x0, matrix products: 30.8 us -> none  [the longest x12 21.5 us: contract(): jnp.einsum(pattern, operand, matrix, preferred_element_type=jnp.float32)]
    all_gather x1 -> x0, waiting for transfers between devices: 30.6 us -> none  [per_device(): arrived = lax.all_gather(hidden, CH, axis=2, tiled=True)]
    all_to_all x2 -> x0, blocking collectives: 18.6 us -> none  [moved_by_axis(): lax.all_to_all(parts, axes[k], split_axis=k, concat_axis=k, tiled=True)]
    all_to_all x3 -> x0, starting transfers between devices: 16.4 us -> none  [the longest x1 8.16 us: channel_plan(): lax.all_to_all(tiled.astype(jnp.bfloat16), 'seq', split_axis=3, concat_ax...]
    convert_element_type x4 -> x1, local copies, waits for them, and re-layouts: 7.76 us -> 1.68 us  [per_device(): pieces = signal.reshape(16, 256, 128).astype(BF16).transpose(2, 0, 1)]
    reduce_sum x1 -> x0, other arithmetic: 6.04 us -> none  [per_device(): return jnp.sum(pieces, axis=2)]
  transfers between devices with their start and end apart: 4 -> 0, of which waited for: 4 -> 0; matrix products, arithmetic and copies ran while one was open for 11% -> 0% of each run, Pallas kernels for 0% -> 0%
where the time goes in v1:
time: 125 us; the launch traced here: 124 us
  Pallas kernels  108 us (86%)
  local copies, waits for them, and re-layouts  9.49 us (8%)
  other arithmetic  6.54 us (5%)
    pallas_call x1, Pallas kernels, per_device(): pl.pallas_call(kernel, out_shape=jax.ShapeDtypeStruct((8, 512, 128), BF16...  108 us
    unnamed x7, local copies, waits for them, and re-layouts  5.35 us
    concatenate x1, other arithmetic, per_device(): source = jnp.concatenate([pieces, filters], 0)  3.17 us
    reshape x1, other arithmetic, per_device(): return result.astype(F32).reshape(1, 4096, 128)  2.68 us

profile of v1, /device:TPU:0, one launch (start us, length us, event | category | flops | bytes accessed | tf_op | source)
XLA Modules:
  0.0 124.3 jit_solution(10369834434324110818)
XLA Ops:
  0.0 5.0 %copy.15 = bf16[2,16,256,128]{2,1,3,0:T(8,128)(2,1)} copy(f32[2,16,256,128]{3,2,1,0:T(8,128)} %param.13) | data formatting | bytes 6291456 | tf_op args[1]
  5.0 0.0 copy-start
  5.0 1.9 %copy.18 = bf16[2,16,256,16,2,4]{2,1,5,0,3,4:T(8,128)(2,1)S(1)} copy(bf16[2,16,256,16,2,4]{2,1,5,4,3,0:T(8,128)(2,1)} %bitcast.13) | data formatting | bytes 4194304 | tf_op jit(solution)/shard_map/reshape | solution.py:359
  6.9 0.3 copy-done
  7.2 0.1 convert_element_type.13
  7.3 1.7 %copy.14 = bf16[16,256,128]{1,0,2:T(8,128)(2,1)} copy(bf16[16,256,128]{2,1,0:T(8,128)(2,1)S(1)} %bitcast.14) | data formatting | bytes 2097152 | tf_op jit(solution)/shard_map/convert_element_type | solution.py:357
  9.0 0.0 copy-start.1
  9.0 0.0 copy-start.2
  9.0 3.2 %pad_maximum_fusion.src = bf16[3,16,2,4,16,256]{5,4,3,2,1,0:T(8,128)(2,1)} fusion(bf16[2,16,2,4,16,256]{5,4,3,2,1,0:T(8,128)(2,1)S(1)} %bitcast.12, bf16[1,16,2,4,16,256]{5,4,3,2,1,0:T(8,128)(2,1)} %bitcast.16), kind=kLoop, calls=%fused_computation | loop fusion | flops 1572864 | bytes 6291456 | tf_op jit(solution)/shard_map/concatenate | solution.py:361
  12.2 0.0 copy-done.1
  12.2 0.6 dynamic-slice_convert_fusion.mode
  12.8 0.0 copy-done.2
  12.8 0.6 dynamic_slice.7.gain
  13.4 108.3 %hyena.1 = bf16[8,512,128]{2,1,0:T(8,128)(2,1)} custom-call(bf16[3,16,2,4,16,256]{5,4,3,2,1,0:T(8,128)(2,1)} %pad_maximum_fusion.src, bf16[128,1024]{1,0:T(8,128)(2,1)} %w.1, f32[8]{0:T(128)} %dynamic-slice_convert_fusion.mode, f32[8]{0:T(128)} %dynamic_slice.7.gain, bf16[512,256]{1,0:T(8,128)(2,1)} %constant.26.clone.first, ...), custom_call_target="tpu_custom_call" | custom-call | tf_op jit(solution)/shard_map/hyena/pallas_call | solution.py:373
  121.6 2.7 %bitcast_convert_fusion = f32[1,4096,128]{2,1,0:T(8,128)} fusion(bf16[1,4096,128]{2,1,0:T(8,128)(2,1)} %bitcast.15), kind=kLoop, calls=%fused_computation.2 | loop fusion | flops 524288 | bytes 3145728 | tf_op jit(solution)/shard_map/reshape | solution.py:409
Async XLA Ops:
  5.0 2.2 %copy-start = (f32[1,4096,128]{2,1,0:T(8,128)S(1)}, f32[1,4096,128]{2,1,0:T(8,128)}, u32[]{:S(2)}) copy-start(f32[1,4096,128]{2,1,0:T(8,128)} %param.12) | copy-start | bytes 6291460
  9.0 3.2 %copy-start.1 = (s32[128]{0:T(128)S(1)}, s32[128]{0:T(128)}, u32[]{:S(2)}) copy-start(s32[128]{0:T(128)} %param.14) | copy-start | bytes 1540
  9.0 3.8 %copy-start.2 = (f32[128]{0:T(128)S(1)}, f32[128]{0:T(128)}, u32[]{:S(2)}) copy-start(f32[128]{0:T(128)} %param.15) | copy-start | bytes 1540

commit v2 on v1

v2 whole, which is shorter than its diff:
```python
import math

import jax
import jax.numpy as jnp
import numpy as np
from jax import lax
from jax.experimental import pallas as pl
from jax.experimental.pallas import tpu as pltpu
from jax.sharding import PartitionSpec as P

ROWS = 256
COLUMNS = 256
LENGTH = 65536
BF16 = jnp.bfloat16
F32 = jnp.float32
MESH = pl.DeviceIdType.MESH


def tables():
    counter = np.arange(256)
    angle = (counter[:, None] * counter[None, :] % 256) * (2.0 * math.pi / 256)
    c, s = np.cos(angle), np.sin(angle)
    first = np.concatenate([c, -s], 0)
    second = np.block([[c, -s], [s, c]])
    third = np.block([[c, s], [-s, c]])
    last = np.concatenate([c, -s], 1) / LENGTH
    twist = counter[:, None] * counter[None, :] * (2.0 * math.pi / LENGTH)
    twist = np.stack([np.cos(twist), np.sin(twist)])
    scatter = np.zeros((256, 256))
    for m in range(4):
        for t in range(4):
            for a in range(16):
                x, k, a2 = a // 4, a // 2 % 2, a % 2
                scatter[t * 64 + ((k * 4 + x) * 2 + a2) * 4 + m, (m * 4 + t) * 16 + a] = 1
    regroup = np.zeros((256, 256))
    for h in range(2):
        for s in range(16):
            for a2 in range(2):
                for m in range(4):
                    regroup[((h * 16 + s) * 2 + a2) * 4 + m, a2 * 128 + s * 8 + h * 4 + m] = 1
    half = [jnp.asarray(t, BF16) for t in (first, second, third, last, scatter, regroup)]
    return half + [jnp.asarray(twist, F32)]


def flip(v, mask):
    if mask == 0:
        return v
    if mask == 1:
        return v + 1 - 2 * lax.rem(v, 2)
    if mask == 2:
        return lax.rem(v + 2, 4)
    return 3 - v


def dot(a, b):
    return jnp.dot(a, b, preferred_element_type=F32)


def kernel(
    sig, spec, w, mode, gain, first, second, third, last, scatter, regroup, twist,
    out,
    rel1, buf, rel2, final, spectral, hid, send, brel1, bbuf, brel2, bfinal,
    swap, xrel, gathered, rows, wfull, prod, swap2, xrel2,
    a_sems, b_sems, w_sems, c_sems, d_sems,
):
    s = lax.axis_index("seq")
    c = lax.axis_index("ch")
    z, y, x, k = s // 4, lax.rem(s, 4), c // 2, lax.rem(c, 2)
    other = 1 - k

    def zdev(mask):
        return {"seq": flip(z, mask) * 4 + y, "ch": c}

    def ydev(mask):
        return {"seq": z * 4 + flip(y, mask), "ch": c}

    def xdev(mask):
        return {"seq": s, "ch": flip(x, mask) * 2 + k}

    partner = {"seq": s, "ch": x * 2 + other}

    def copy(a, b, ss, rs, dev):
        return pltpu.make_async_remote_copy(a, b, ss, rs, device_id=dev, device_id_type=MESH)

    def recv(ref, sem):
        copy(ref, ref, sem, sem, partner).wait_recv()

    def sent(ref, sem):
        copy(ref, ref, sem, sem, partner).wait_send()

    barrier = pltpu.get_barrier_semaphore()
    for dev in (zdev(1), zdev(3), ydev(1), ydev(3), xdev(1), xdev(3), partner):
        pl.semaphore_signal(barrier, 1, device_id=dev, device_id_type=MESH)
    pl.semaphore_wait(barrier, 7)

    class Plane:
        def __init__(self, grab, rel1, buf, rel2, final, sems):
            self.grab, self.rel1, self.buf, self.rel2, self.final = grab, rel1, buf, rel2, final
            self.s1, self.s2, self.rrel1, self.rfin, self.rbuf, self.rrel2 = sems

        def dev(self, u, leg, mask):
            return zdev(mask) if u % 2 == leg else ydev(mask)

        def slot(self, u, m1, m2):
            if u % 2 == 0:
                return self.final.at[u, flip(z, m1), flip(y, m2)]
            return self.final.at[u, flip(z, m2), flip(y, m1)]

        def row(self, u, mask):
            if u % 2 == 0:
                return self.grab(u, flip(z, mask), slice(None))
            return self.grab(u, slice(None), flip(y, mask))

        def F(self, u):
            one, three = self.dev(u, 0, 1), self.dev(u, 0, 3)
            s1, rb = self.s1.at[u], self.rbuf
            copy(self.row(u, 2), self.rel1.at[u], s1, self.rrel1.at[u], one).start()
            copy(self.row(u, 3), self.buf.at[u, 2], s1, rb.at[u, 2], three).start()
            copy(self.row(u, 1), self.buf.at[u, 0], s1, rb.at[u, 0], one).start()

        def R(self, u):
            recv(self.rel1.at[u], self.rrel1.at[u])
            three = self.dev(u, 0, 3)
            copy(
                self.rel1.at[u], self.buf.at[u, 1], self.s1.at[u], self.rbuf.at[u, 1], three
            ).start()

        def S(self, u, m1):
            if m1:
                recv(self.buf.at[u, m1 - 1], self.rbuf.at[u, m1 - 1])

            def part(mask):
                other = flip(y if u % 2 == 0 else z, mask)
                if m1:
                    return self.buf.at[u, m1 - 1, other]
                return self.grab(u, z, other) if u % 2 == 0 else self.grab(u, other, y)

            slot = self.slot(u, m1, 0)
            one, three = self.dev(u, 1, 1), self.dev(u, 1, 3)
            s2, done = self.s2.at[u], self.rfin.at[u]
            copy(part(2), self.rel2.at[u, m1], s2, self.rrel2.at[u, m1], one).start()
            copy(part(3), slot, s2, done, three).start()
            copy(part(1), slot, s2, done, one).start()
            slot[...] = part(0)[...]

        def T(self, u, m1):
            recv(self.rel2.at[u, m1], self.rrel2.at[u, m1])
            slot = self.slot(u, m1, 1)
            three = self.dev(u, 1, 3)
            copy(self.rel2.at[u, m1], slot, self.s2.at[u], self.rfin.at[u], three).start()

        def done(self, u):
            recv(self.final.at[u, pl.ds(0, 3)], self.rfin.at[u])

        def drain(self, u):
            sent(self.final.at[u], self.s1.at[u])
            sent(self.final.at[u], self.s2.at[u])

    def grab_inputs(u, zi, yi):
        if u < 2:
            return sig.at[zi, yi, u]
        return spec.at[u % 2, zi, yi, u // 2 - 1]

    A = Plane(grab_inputs, rel1, buf, rel2, final, a_sems)
    B = Plane(lambda u, zi, yi: send.at[u, zi, yi], brel1, bbuf, brel2, bfinal, b_sems)

    def twists(ch):
        on = mode[s * 8 + ch] == 1
        return jnp.where(on, twist[0], 1.0), jnp.where(on, twist[1], 0.0)

    def forward(h, lo):
        def step(m, carry):
            image = final[h, :, :, m].reshape(256, 256)
            value = dot(first[...], image)
            re, im = value[:256], value[256:]
            tc, ts = twists(4 * h + m)
            pair = jnp.concatenate([re * tc + im * ts, im * tc - re * ts], 1).astype(BF16)
            spectral[4 * h + m] = dot(pair, second[...])
            return carry

        lax.fori_loop(lo, lo + 2, step, 0)

    def inverse(h, lo):
        def step(m, carry):
            value = spectral[4 * h + m]
            re, im = value[:, :256], value[:, 256:]
            fr = final[2 + 2 * h, :, :, m].reshape(256, 256).astype(F32)
            fi = final[3 + 2 * h, :, :, m].reshape(256, 256).astype(F32)
            pair = jnp.concatenate([re * fr - im * fi, re * fi + im * fr], 1).astype(BF16)
            value = dot(pair, third[...])
            re, im = value[:, :256], value[:, 256:]
            tc, ts = twists(4 * h + m)
            pair = jnp.concatenate([re * tc - im * ts, re * ts + im * tc], 0).astype(BF16)
            value = dot(last[...], pair)
            image = final[h, :, :, m].reshape(256, 256).astype(F32)
            value = value + gain[s * 8 + 4 * h + m] * image
            hid[m] = value.astype(BF16).reshape(4, 4, 16, 256)
            return carry

        lax.fori_loop(lo, lo + 2, step, 0)

    def place(h):
        for t in range(4):
            block = hid[:, t].reshape(256, 256)
            send[h, t] = dot(scatter[...], block).astype(BF16).reshape(4, 2, 4, 8, 256)

    own = pl.ds(pl.multiple_of(c * 128, 128), 128)

    def wrows(mask):
        return wfull.at[pl.ds(pl.multiple_of((flip(x, mask) * 2 + k) * 128, 128), 128)]

    ws, wx, wp = w_sems

    def pair(method, u, *m):
        method(u, *m)
        method(u + 1, *m)

    pair(A.F, 0)
    pair(A.S, 0, 0)
    pair(A.F, 2)
    copy(w, wfull.at[own], ws, wx.at[0], xdev(1)).start()
    copy(w, wfull.at[own], ws, wx.at[2], xdev(3)).start()
    copy(w, wfull.at[own], ws, wp.at[0], partner).start()
    wfull[own] = w[...]
    pair(A.R, 0)
    pair(A.F, 4)
    pair(A.S, 0, 3)
    pair(A.T, 0, 0)
    pair(A.S, 2, 0)
    pair(A.S, 0, 1)
    pair(A.T, 0, 3)
    pair(A.R, 2)
    pair(A.S, 0, 2)
    pair(A.T, 0, 1)
    recv(wrows(1), wx.at[0])
    copy(wrows(1), wrows(1), ws, wx.at[1], xdev(3)).start()
    copy(wrows(1), wrows(1), ws, wp.at[1], partner).start()
    pair(A.S, 2, 3)
    pair(A.T, 2, 0)
    pair(A.S, 4, 0)
    pair(A.T, 0, 2)
    recv(wrows(3), wx.at[2])
    copy(wrows(3), wrows(3), ws, wp.at[3], partner).start()
    pair(A.R, 4)
    pair(A.S, 2, 1)
    pair(A.T, 2, 3)
    A.done(0)
    forward(0, 0)
    pair(A.S, 2, 2)
    pair(A.T, 2, 1)
    recv(wrows(2), wx.at[1])
    copy(wrows(2), wrows(2), ws, wp.at[2], partner).start()
    pair(A.S, 4, 3)
    forward(0, 2)
    pair(A.T, 4, 0)
    pair(A.T, 2, 2)
    A.done(1)
    forward(1, 0)
    pair(A.S, 4, 1)
    pair(A.T, 4, 3)
    forward(1, 2)
    pair(A.S, 4, 2)
    A.done(2)
    A.done(3)
    inverse(0, 0)
    pair(A.T, 4, 1)
    inverse(0, 2)
    pair(A.T, 4, 2)
    place(0)
    B.F(0)
    B.S(0, 0)
    A.done(4)
    A.done(5)
    inverse(1, 0)
    B.R(0)
    B.S(0, 3)
    B.T(0, 0)
    inverse(1, 2)
    place(1)
    B.F(1)
    B.S(1, 0)
    B.S(0, 1)
    B.T(0, 3)
    B.S(0, 2)
    B.R(1)
    B.T(0, 1)
    B.S(1, 3)
    B.T(1, 0)
    B.T(0, 2)

    es, er, xs, xr, fr = c_sems

    def xsend(h, i):
        kept = k if i == 0 else other

        def part(mask):
            if i == 0:
                return bfinal.at[h, :, :, k, flip(x, mask)]
            return swap.at[h, :, :, flip(x, mask)]

        slot = gathered.at[x, kept, h]
        copy(part(2), xrel.at[h, i], xs, xr.at[h, i], xdev(1)).start()
        copy(part(3), slot, xs, fr, xdev(3)).start()
        copy(part(1), slot, xs, fr, xdev(1)).start()
        slot[...] = part(0)[...]

    def xfwd(h, i):
        kept = k if i == 0 else other
        recv(xrel.at[h, i], xr.at[h, i])
        copy(xrel.at[h, i], gathered.at[flip(x, 1), kept, h], xs, fr, xdev(3)).start()

    def exchange(h):
        B.done(h)
        copy(bfinal.at[h, :, :, other], swap.at[h], es, er.at[h], partner).start()
        xsend(h, 0)

    exchange(0)
    B.S(1, 1)
    B.T(1, 3)
    recv(swap.at[0], er.at[0])
    xsend(0, 1)
    B.S(1, 2)
    B.T(1, 1)
    xfwd(0, 0)
    B.T(1, 2)
    xfwd(0, 1)
    exchange(1)
    recv(swap.at[1], er.at[1])
    xsend(1, 1)
    xfwd(1, 0)
    xfwd(1, 1)
    for mask in range(4):
        recv(wfull.at[pl.ds(0, 128)], wp.at[mask])
    recv(gathered.at[pl.ds(0, 3)], fr)

    for i in range(8):
        block = gathered[i // 2, i % 2].reshape(256, 256)
        value = lax.dot_general(
            block, regroup[...], (((0,), (0,)), ((), ())), preferred_element_type=F32
        ).astype(BF16)
        rows[0, :, i * 128 : (i + 1) * 128] = value[:, :128]
        rows[1, :, i * 128 : (i + 1) * 128] = value[:, 128:]

    for i in range(4):
        value = dot(rows[...].reshape(512, 1024), wfull[:, i * 256 : (i + 1) * 256]).astype(BF16)
        prod[0, i] = value[:, :128]
        prod[1, i] = value[:, 128:]

    ds, dr, dxs, dxr, dout = d_sems
    copy(prod.at[other], swap2, ds, dr, partner).start()

    def osend(i):
        kept = k if i == 0 else other

        def part(mask):
            if i == 0:
                return prod.at[k, flip(x, mask)]
            return swap2.at[flip(x, mask)]

        slot = out.at[x * 2 + kept]
        copy(part(2), xrel2.at[i], dxs, dxr.at[i], xdev(1)).start()
        copy(part(3), slot, dxs, dout, xdev(3)).start()
        copy(part(1), slot, dxs, dout, xdev(1)).start()
        slot[...] = part(0)[...]

    def ofwd(i):
        kept = k if i == 0 else other
        recv(xrel2.at[i], dxr.at[i])
        copy(xrel2.at[i], out.at[flip(x, 1) * 2 + kept], dxs, dout, xdev(3)).start()

    osend(0)
    recv(swap2, dr)
    osend(1)
    ofwd(0)
    ofwd(1)
    recv(out.at[pl.ds(0, 6)], dout)

    for u in range(6):
        A.drain(u)
    for h in range(2):
        B.drain(h)
    sent(wfull.at[pl.ds(0, 7 * 128)], ws)
    sent(swap, es)
    sent(gathered, xs)
    sent(swap2, ds)
    sent(out, dxs)


def per_device(signal, spectrum, channel_mode, skip_gain, out_weight):
    pieces = signal.reshape(16, 256, 128).astype(BF16).transpose(2, 0, 1)
    pieces = pieces.reshape(4, 4, 2, 4, 16, 256)
    filters = spectrum.astype(BF16).transpose(0, 3, 1, 2)
    filters = filters.reshape(2, 4, 4, 2, 4, 16, 256)
    unit = (4, 16, 256)
    small = (2, 4, 8, 256)
    dma = pltpu.SemaphoreType.DMA

    def plane(n):
        return (dma((n,)), dma((n,)), dma((n,)), dma((n,)), dma((n, 3)), dma((n, 4)))

    vmem = pl.BlockSpec(memory_space=pltpu.VMEM)
    smem = pl.BlockSpec(memory_space=pltpu.SMEM)
    result = pl.pallas_call(
        kernel,
        out_shape=jax.ShapeDtypeStruct((8, 512, 128), BF16),
        in_specs=[vmem, vmem, vmem, smem, smem] + [vmem] * 7,
        out_specs=vmem,
        scratch_shapes=[
            pltpu.VMEM((6, 4) + unit, BF16),
            pltpu.VMEM((6, 3, 4) + unit, BF16),
            pltpu.VMEM((6, 4) + unit, BF16),
            pltpu.VMEM((6, 4, 4) + unit, BF16),
            pltpu.VMEM((8, 256, 512), F32),
            pltpu.VMEM((4, 4, 4, 16, 256), BF16),
            pltpu.VMEM((2, 4, 4) + small, BF16),
            pltpu.VMEM((2, 4) + small, BF16),
            pltpu.VMEM((2, 3, 4) + small, BF16),
            pltpu.VMEM((2, 4) + small, BF16),
            pltpu.VMEM((2, 4, 4) + small, BF16),
            pltpu.VMEM((2, 4, 4, 4, 8, 256), BF16),
            pltpu.VMEM((2, 2, 4, 4, 8, 256), BF16),
            pltpu.VMEM((4, 2, 2, 4, 4, 8, 256), BF16),
            pltpu.VMEM((2, 256, 1024), BF16),
            pltpu.VMEM((1024, 1024), BF16),
            pltpu.VMEM((2, 4, 512, 128), BF16),
            pltpu.VMEM((4, 512, 128), BF16),
            pltpu.VMEM((2, 512, 128), BF16),
            plane(6),
            plane(2),
            (dma, dma((3,)), dma((4,))),
            (dma, dma((2,)), dma, dma((2, 2)), dma),
            (dma, dma, dma, dma((2,)), dma),
        ],
        compiler_params=pltpu.CompilerParams(
            collective_id=0, has_side_effects=True, vmem_limit_bytes=40 << 20
        ),
        name="hyena",
    )(pieces, filters, out_weight, channel_mode, skip_gain, *tables())
    return result.astype(F32).reshape(1, 4096, 128)


def solution(mesh):
    in_specs = (
        P(None, "seq", "ch"), P(None, "seq", None, "ch"), P("ch"), P("ch"), P("ch", None)
    )
    return jax.shard_map(
        per_device, mesh=mesh, in_specs=in_specs, out_specs=P(None, "seq", "ch"), check_vma=False
    )
```

time: 125 us -> 120 us (0.960)
  Pallas kernels: 108 us -> 100 us
  local copies, waits for them, and re-layouts: 9.49 us -> 11.1 us
  other arithmetic: 6.54 us -> 7.99 us
    pallas_call x1, Pallas kernels: 108 us -> 100 us  [per_device(): pl.pallas_call(kernel, out_shape=jax.ShapeDtypeStruct((8, 512, 128), BF16...]
    transpose x0 -> x1, other arithmetic: none -> 3.83 us  [per_device(): filters = spectrum.astype(BF16).transpose(0, 3, 1, 2)]
    transpose x0 -> x1, local copies, waits for them, and re-layouts: none -> 3.34 us  [per_device(): filters = spectrum.astype(BF16).transpose(0, 3, 1, 2)]
    concatenate x1 -> x0, other arithmetic: 3.17 us -> none  [per_device(): source = jnp.concatenate([pieces, filters], 0)]
    convert_element_type x1, other arithmetic: 0.1 us -> 2.71 us  [per_device(): pieces = signal.reshape(16, 256, 128).astype(BF16).transpose(2, 0, 1)]
    reshape x1 -> x0, local copies, waits for them, and re-layouts: 1.88 us -> none  [per_device(): filters = spectrum.astype(BF16).reshape(2, 16, 256, 16, 2, 4)]
    unnamed x7 -> x20, local copies, waits for them, and re-layouts: 5.35 us -> 5.95 us
where the time goes in v2:
time: 120 us; the launch traced here: 119 us
  Pallas kernels  100 us (83%)
  local copies, waits for them, and re-layouts  11.1 us (9%)
  other arithmetic  7.99 us (7%)
    pallas_call x1, Pallas kernels, per_device(): pl.pallas_call(kernel, out_shape=jax.ShapeDtypeStruct((8, 512, 128), BF16...  100 us
    unnamed x20, local copies, waits for them, and re-layouts  5.95 us
    transpose x1, other arithmetic, per_device(): filters = spectrum.astype(BF16).transpose(0, 3, 1, 2)  3.83 us
    transpose x1, local copies, waits for them, and re-layouts, per_device(): filters = spectrum.astype(BF16).transpose(0, 3, 1, 2)  3.34 us
    convert_element_type x1, other arithmetic, per_device(): pieces = signal.reshape(16, 256, 128).astype(BF16).transpose(2, 0, 1)  2.71 us

profile of v2, /device:TPU:0, one launch (start us, length us, event | category | flops | bytes accessed | tf_op | source)
XLA Modules:
  0.0 119.2 jit_solution(2027332985646005348)
XLA Ops:
  0.0 3.8 %convert_bitcast_fusion = bf16[2,128,16,256]{1,3,2,0:T(8,128)(2,1)} fusion(f32[2,16,256,128]{3,2,1,0:T(8,128)} %param.13), kind=kLoop, calls=%fused_computation | loop fusion | flops 1048576 | bytes 6291456 | tf_op jit(solution)/shard_map/transpose | solution.py:392
  3.8 3.3 %copy.14 = bf16[2,128,16,256]{3,2,1,0:T(8,128)(2,1)S(1)} copy(bf16[2,128,16,256]{1,3,2,0:T(8,128)(2,1)} %convert_bitcast_fusion) | data formatting | bytes 4194304 | tf_op jit(solution)/shard_map/transpose | solution.py:392
  7.2 0.0 copy-start.3
  7.2 0.0 copy-start.6
  7.2 0.0 copy-start.8
  7.2 0.0 copy-start.9
  7.2 2.7 %convert_element_type.10 = bf16[1,4096,128]{2,1,0:T(8,128)(2,1)} convert(f32[1,4096,128]{2,1,0:T(8,128)} %param.12) | non-fusion elementwise | flops 524288 | bytes 3145728 | tf_op jit(solution)/shard_map/convert_element_type | solution.py:390
  9.9 1.9 %copy.13 = bf16[16,256,128]{1,0,2:T(8,128)(2,1)S(1)} copy(bf16[16,256,128]{2,1,0:T(8,128)(2,1)} %bitcast.14) | data formatting | bytes 2097152 | tf_op jit(solution)/shard_map/convert_element_type | solution.py:390
  11.8 0.0 copy-done.3
  11.8 0.0 copy-done.6
  11.8 0.0 copy-done.8
  11.8 0.0 copy-done.9
  11.8 0.0 copy-start
  11.8 1.0 copy-done
  12.9 0.0 copy-start.1
  12.9 1.0 copy-done.1
  13.9 0.0 copy-start.2
  13.9 1.0 copy-done.2
  15.0 0.0 copy-start.4
  15.0 0.9 copy-done.4
  15.9 0.0 copy-start.5
  15.9 0.9 copy-done.5
  16.9 0.0 copy-start.7
  16.9 0.9 copy-done.7
  17.8 100.0 %hyena.1 = bf16[8,512,128]{2,1,0:T(8,128)(2,1)S(1)} custom-call(bf16[4,4,2,4,16,256]{5,4,3,2,1,0:T(8,128)(2,1)S(1)} %bitcast.13, bf16[2,4,4,2,4,16,256]{6,5,4,3,2,1,0:T(8,128)(2,1)S(1)} %bitcast.11, bf16[128,1024]{1,0:T(8,128)(2,1)S(1)} %copy-done.3, s32[128]{0:T(128)S(1)} %copy-done.8, f32[128]{0:T(128)S(1)} %copy-done.9, bf16[512,256]{1,0:T(8,128)(2,1)S(1)} %copy-done.4, ...), custom_call_target="tpu_custom_call" | custom-call | tf_op jit(solution)/shard_map/hyena/pallas_call | solution.py:403
  117.8 1.5 %bitcast_convert_fusion = f32[1,4096,128]{2,1,0:T(8,128)} fusion(bf16[1,4096,128]{2,1,0:T(8,128)(2,1)S(1)} %bitcast.12), kind=kLoop, calls=%fused_computation.1 | loop fusion | flops 524288 | bytes 3145728 | tf_op jit(solution)/shard_map/reshape | solution.py:439
Async XLA Ops:
  7.2 4.6 %copy-start.3 = (bf16[128,1024]{1,0:T(8,128)(2,1)S(1)}, bf16[128,1024]{1,0:T(8,128)(2,1)}, u32[]{:S(2)}) copy-start(bf16[128,1024]{1,0:T(8,128)(2,1)} %w.1) | copy-start | bytes 786436
  7.2 4.6 %copy-start.6 = (bf16[256,256]{1,0:T(8,128)(2,1)S(1)}, bf16[256,256]{1,0:T(8,128)(2,1)}, u32[]{:S(2)}) copy-start(bf16[256,256]{1,0:T(8,128)(2,1)} %constant.18.clone.scatter) | copy-start | bytes 393220
  7.2 4.6 %copy-start.8 = (s32[128]{0:T(128)S(1)}, s32[128]{0:T(128)}, u32[]{:S(2)}) copy-start(s32[128]{0:T(128)} %mode.1) | copy-start | bytes 1540
  7.2 4.6 %copy-start.9 = (f32[128]{0:T(128)S(1)}, f32[128]{0:T(128)}, u32[]{:S(2)}) copy-start(f32[128]{0:T(128)} %gain.1) | copy-start | bytes 1540
  11.8 1.0 copy-start
  12.9 1.0 copy-start.1
  13.9 1.0 copy-start.2
  15.0 0.9 copy-start.4
  15.9 0.9 copy-start.5
  16.9 0.9 copy-start.7

commit v3 on v2

v3 whole, which is shorter than its diff:
```python
import math

import jax
import jax.numpy as jnp
import numpy as np
from jax import lax
from jax.experimental import pallas as pl
from jax.experimental.pallas import tpu as pltpu
from jax.sharding import PartitionSpec as P

ROWS = 256
COLUMNS = 256
LENGTH = 65536
BF16 = jnp.bfloat16
F32 = jnp.float32
MESH = pl.DeviceIdType.MESH


def tables():
    counter = np.arange(256)
    angle = (counter[:, None] * counter[None, :] % 256) * (2.0 * math.pi / 256)
    c, s = np.cos(angle), np.sin(angle)
    first = np.concatenate([c, -s], 0)
    second = np.block([[c, -s], [s, c]])
    third = np.block([[c, s], [-s, c]])
    last = np.concatenate([c, -s], 1) / LENGTH
    twist = counter[:, None] * counter[None, :] * (2.0 * math.pi / LENGTH)
    twist = np.stack([np.cos(twist), np.sin(twist)])
    scatter = np.zeros((256, 256))
    for m in range(4):
        for t in range(4):
            for a in range(16):
                x, k, a2 = a // 4, a // 2 % 2, a % 2
                scatter[t * 64 + ((k * 4 + x) * 2 + a2) * 4 + m, (m * 4 + t) * 16 + a] = 1
    regroup = np.zeros((256, 256))
    for h in range(2):
        for s in range(16):
            for a2 in range(2):
                for m in range(4):
                    regroup[((h * 16 + s) * 2 + a2) * 4 + m, a2 * 128 + s * 8 + h * 4 + m] = 1
    half = [jnp.asarray(t, BF16) for t in (first, second, third, last, scatter, regroup)]
    return half + [jnp.asarray(twist, F32)]


def flip(v, mask):
    if mask == 0:
        return v
    if mask == 1:
        return v + 1 - 2 * lax.rem(v, 2)
    if mask == 2:
        return lax.rem(v + 2, 4)
    return 3 - v


def dot(a, b):
    return jnp.dot(a, b, preferred_element_type=F32)


def kernel(
    sig, spec, w, mode, gain, *refs
):
    tables_hbm, (
        out, first, second, third, last, scatter, regroup, twist,
        buf, final, spectral, hid, send, gathered, rows, wfull, prod,
        t_sems, a_sems, b_sems, w_sems, d_sems, met,
    ) = refs[:7], refs[7:]
    s = lax.axis_index("seq")
    c = lax.axis_index("ch")
    z, y, x, k = s // 4, lax.rem(s, 4), c // 2, lax.rem(c, 2)
    other = 1 - k

    def zdev(mask):
        return {"seq": flip(z, mask) * 4 + y, "ch": c}

    def ydev(mask):
        return {"seq": z * 4 + flip(y, mask), "ch": c}

    def xdev(mask):
        return {"seq": s, "ch": flip(x, mask) * 2 + k}

    partner = {"seq": s, "ch": x * 2 + other}

    def copy(a, b, ss, rs, dev):
        return pltpu.make_async_remote_copy(a, b, ss, rs, device_id=dev, device_id_type=MESH)

    def recv(ref, sem):
        copy(ref, ref, sem, sem, partner).wait_recv()

    def sent(ref, sem):
        copy(ref, ref, sem, sem, partner).wait_send()

    def peers(fn):
        for mask in (2, 1, 3, 0):
            for core in (k, other):
                if mask or core is other:
                    fn(flip(x, mask) * 2 + core)

    copies = [
        pltpu.make_async_copy(a, b, t_sems.at[i])
        for i, (a, b) in enumerate(
            zip(tables_hbm, (first, second, third, last, scatter, regroup, twist))
        )
    ]
    for t in copies:
        t.start()

    barrier = pltpu.get_barrier_semaphore()

    def greet(dev):
        pl.semaphore_signal(barrier, 1, device_id=dev, device_id_type=MESH)

    for mask in (1, 2, 3):
        greet(zdev(mask))
        greet(ydev(mask))
    peers(lambda t: greet({"seq": s, "ch": t}))
    pl.semaphore_wait(barrier, 13)

    class Plane:
        def __init__(self, grab, buf, final, sems):
            self.grab, self.buf, self.final = grab, buf, final
            self.s1, self.s2, self.rfin, self.rbuf = sems

        def dev(self, u, leg, mask):
            return zdev(mask) if u % 2 == leg else ydev(mask)

        def F(self, u):
            for mask in (2, 1, 3):
                if u % 2 == 0:
                    row = self.grab(u, flip(z, mask), slice(None))
                else:
                    row = self.grab(u, slice(None), flip(y, mask))
                to, sem = self.buf.at[u, mask - 1], self.rbuf.at[u, mask - 1]
                copy(row, to, self.s1.at[u], sem, self.dev(u, 0, mask)).start()

        def S(self, u, m1):
            if m1:
                recv(self.buf.at[u, m1 - 1], self.rbuf.at[u, m1 - 1])
            for mask in (2, 1, 3, 0):
                other = flip(y if u % 2 == 0 else z, mask)
                if m1:
                    part = self.buf.at[u, m1 - 1, other]
                else:
                    part = self.grab(u, z, other) if u % 2 == 0 else self.grab(u, other, y)
                if u % 2 == 0:
                    slot = self.final.at[u, flip(z, m1), y]
                else:
                    slot = self.final.at[u, z, flip(y, m1)]
                if mask:
                    to = self.dev(u, 1, mask)
                    copy(part, slot, self.s2.at[u], self.rfin.at[u], to).start()
                else:
                    slot[...] = part[...]

        def done(self, u):
            recv(self.final.at[u, pl.ds(0, 3)], self.rfin.at[u])

        def drain(self, u):
            sent(self.final.at[u, pl.ds(0, 3)], self.s1.at[u])
            sent(self.final.at[u, pl.ds(0, 3)], self.s2.at[u])

    def grab_inputs(u, zi, yi):
        if u < 2:
            return sig.at[zi, yi, u]
        return spec.at[u % 2, zi, yi, u // 2 - 1]

    A = Plane(grab_inputs, buf, final, a_sems)

    def twists(ch):
        on = mode[s * 8 + ch] == 1
        return jnp.where(on, twist[0], 1.0), jnp.where(on, twist[1], 0.0)

    def forward(h, lo):
        def step(m, carry):
            image = final[h, :, :, m].reshape(256, 256)
            value = dot(first[...], image)
            re, im = value[:256], value[256:]
            tc, ts = twists(4 * h + m)
            pair = jnp.concatenate([re * tc + im * ts, im * tc - re * ts], 1).astype(BF16)
            spectral[4 * h + m] = dot(pair, second[...])
            return carry

        lax.fori_loop(lo, lo + 2, step, 0)

    def inverse(h, lo):
        def step(m, carry):
            value = spectral[4 * h + m]
            re, im = value[:, :256], value[:, 256:]
            fr = final[2 + 2 * h, :, :, m].reshape(256, 256).astype(F32)
            fi = final[3 + 2 * h, :, :, m].reshape(256, 256).astype(F32)
            pair = jnp.concatenate([re * fr - im * fi, re * fi + im * fr], 1).astype(BF16)
            value = dot(pair, third[...])
            re, im = value[:, :256], value[:, 256:]
            tc, ts = twists(4 * h + m)
            pair = jnp.concatenate([re * tc - im * ts, re * ts + im * tc], 0).astype(BF16)
            value = dot(last[...], pair)
            image = final[h, :, :, m].reshape(256, 256).astype(F32)
            value = value + gain[s * 8 + 4 * h + m] * image
            hid[m] = value.astype(BF16).reshape(4, 4, 16, 256)
            return carry

        lax.fori_loop(lo, lo + 2, step, 0)

    def place(h):
        for t in range(4):
            block = hid[:, t].reshape(256, 256)
            value = dot(scatter[...], block).astype(BF16)
            send[h, t * 32 : (t + 1) * 32] = value.reshape(32, 8, 256)

    sb, rb = b_sems
    mine = c * 16 + s

    def scatter_all(h):
        def step(i, carry):
            zz, yy = lax.rem(z + lax.rem(i, 4), 4), lax.rem(y + i // 4, 4)
            block = (zz * 4 + yy) * 8
            for mask in (2, 1, 3, 0):
                for core in (k, other):
                    xx = flip(x, mask)
                    part = send.at[h, block + core * 4 + xx]
                    to = {"seq": zz * 4 + yy, "ch": xx * 2 + core}
                    one = copy(part, gathered.at[h, mine], sb.at[h], rb.at[h], to)
                    if mask == 0 and core is k:

                        @pl.when(i > 0)
                        def _():
                            one.start()

                    else:
                        one.start()
            return carry

        lax.fori_loop(0, 16, step, 0)
        gathered[h, mine] = send[h, s * 8 + k * 4 + x]

    own = pl.ds(pl.multiple_of(c * 128, 128), 128)
    ws, wr = w_sems

    def pair(method, u, *m):
        method(u, *m)
        method(u + 1, *m)

    pair(A.F, 0)
    pair(A.F, 2)
    pair(A.S, 0, 0)
    pair(A.S, 2, 0)
    pair(A.F, 4)
    peers(lambda t: copy(w, wfull.at[own], ws, wr, {"seq": s, "ch": t}).start())
    wfull[own] = w[...]
    pair(A.S, 0, 1)
    pair(A.S, 0, 3)
    pair(A.S, 0, 2)
    pair(A.S, 2, 1)
    pair(A.S, 2, 3)
    pair(A.S, 2, 2)
    pair(A.S, 4, 0)
    A.done(0)
    for t in copies:
        t.wait()
    forward(0, 0)
    pair(A.S, 4, 1)
    forward(0, 2)
    A.done(1)
    peers(
        lambda t: pl.semaphore_signal(
            met, 1, device_id={"seq": s, "ch": t}, device_id_type=MESH
        )
    )
    forward(1, 0)
    pair(A.S, 4, 3)
    forward(1, 2)
    pair(A.S, 4, 2)
    A.done(2)
    A.done(3)
    inverse(0, 0)
    inverse(0, 2)
    place(0)
    pl.semaphore_wait(met, 7)
    scatter_all(0)
    A.done(4)
    A.done(5)
    inverse(1, 0)
    inverse(1, 2)
    place(1)
    scatter_all(1)
    recv(wfull.at[pl.ds(0, 7 * 128)], wr)
    recv(gathered.at[0, pl.ds(0, 127)], rb.at[0])
    recv(gathered.at[1, pl.ds(0, 127)], rb.at[1])

    for i in range(8):
        block = jnp.concatenate(
            [gathered[h, 16 * i : 16 * i + 16].reshape(128, 256) for h in range(2)], 0
        )
        value = lax.dot_general(
            block, regroup[...], (((0,), (0,)), ((), ())), preferred_element_type=F32
        ).astype(BF16)
        rows[0, :, i * 128 : (i + 1) * 128] = value[:, :128]
        rows[1, :, i * 128 : (i + 1) * 128] = value[:, 128:]

    for i in range(4):
        value = dot(rows[...].reshape(512, 1024), wfull[:, i * 256 : (i + 1) * 256]).astype(BF16)
        prod[0, i] = value[:, :128]
        prod[1, i] = value[:, 128:]

    ds, dr = d_sems

    def give(t):
        part = prod.at[lax.rem(t, 2), t // 2]
        copy(part, out.at[c], ds, dr, {"seq": s, "ch": t}).start()

    peers(give)
    out[c] = prod[k, x]
    recv(out.at[pl.ds(0, 7)], dr)

    for u in range(6):
        A.drain(u)
    for h in range(2):
        sent(send.at[h, pl.ds(0, 127)], sb.at[h])
    sent(wfull.at[pl.ds(0, 7 * 128)], ws)
    sent(out.at[pl.ds(0, 7)], ds)


def per_device(signal, spectrum, channel_mode, skip_gain, out_weight):
    pieces = signal.reshape(16, 256, 128).astype(BF16).transpose(2, 0, 1)
    pieces = pieces.reshape(4, 4, 2, 4, 16, 256)
    filters = spectrum.astype(BF16).transpose(0, 3, 1, 2)
    filters = filters.reshape(2, 4, 4, 2, 4, 16, 256)
    unit = (4, 16, 256)
    dma = pltpu.SemaphoreType.DMA
    constants = tables()
    anywhere = pl.BlockSpec(memory_space=pltpu.HBM)
    vmem = pl.BlockSpec(memory_space=pltpu.VMEM)
    smem = pl.BlockSpec(memory_space=pltpu.SMEM)
    result = pl.pallas_call(
        kernel,
        out_shape=jax.ShapeDtypeStruct((8, 512, 128), BF16),
        in_specs=[vmem, vmem, vmem, smem, smem] + [anywhere] * 7,
        out_specs=vmem,
        scratch_shapes=[
            *(pltpu.VMEM(t.shape, t.dtype) for t in constants),
            pltpu.VMEM((6, 3, 4) + unit, BF16),
            pltpu.VMEM((6, 4, 4) + unit, BF16),
            pltpu.VMEM((8, 256, 512), F32),
            pltpu.VMEM((4, 4, 4, 16, 256), BF16),
            pltpu.VMEM((2, 128, 8, 256), BF16),
            pltpu.VMEM((2, 128, 8, 256), BF16),
            pltpu.VMEM((2, 256, 1024), BF16),
            pltpu.VMEM((1024, 1024), BF16),
            pltpu.VMEM((2, 4, 512, 128), BF16),
            dma((7,)),
            (dma((6,)), dma((6,)), dma((6,)), dma((6, 3))),
            (dma((2,)), dma((2,))),
            (dma, dma),
            (dma, dma),
            pltpu.SemaphoreType.REGULAR,
        ],
        compiler_params=pltpu.CompilerParams(
            collective_id=0, has_side_effects=True, vmem_limit_bytes=40 << 20
        ),
        name="hyena",
    )(pieces, filters, out_weight, channel_mode, skip_gain, *constants)
    return result.astype(F32).reshape(1, 4096, 128)


def solution(mesh):
    in_specs = (
        P(None, "seq", "ch"), P(None, "seq", None, "ch"), P("ch"), P("ch"), P("ch", None)
    )
    return jax.shard_map(
        per_device, mesh=mesh, in_specs=in_specs, out_specs=P(None, "seq", "ch"), check_vma=False
    )
```

time: 120 us -> 93.4 us (0.78)
  Pallas kernels: 100 us -> 72.7 us
    pallas_call x1, Pallas kernels: 100 us -> 72.7 us  [per_device(): pl.pallas_call(kernel, out_shape=jax.ShapeDtypeStruct((8, 512, 128), BF16...]
where the time goes in v3:
time: 93.4 us; the launch traced here: 91.9 us
  Pallas kernels  72.7 us (78%)
  local copies, waits for them, and re-layouts  11.1 us (12%)
  other arithmetic  7.99 us (9%)
    pallas_call x1, Pallas kernels, per_device(): pl.pallas_call(kernel, out_shape=jax.ShapeDtypeStruct((8, 512, 128), BF16...  72.7 us
    unnamed x20, local copies, waits for them, and re-layouts  5.95 us
    transpose x1, other arithmetic, per_device(): filters = spectrum.astype(BF16).transpose(0, 3, 1, 2)  3.83 us
    transpose x1, local copies, waits for them, and re-layouts, per_device(): filters = spectrum.astype(BF16).transpose(0, 3, 1, 2)  3.34 us
    convert_element_type x1, other arithmetic, per_device(): pieces = signal.reshape(16, 256, 128).astype(BF16).transpose(2, 0, 1)  2.71 us

profile of v3, /device:TPU:0, one launch (start us, length us, event | category | flops | bytes accessed | tf_op | source)
XLA Modules:
  0.0 91.9 jit_solution(12086121895281353181)
XLA Ops:
  0.0 3.8 %convert_bitcast_fusion = bf16[2,128,16,256]{1,3,2,0:T(8,128)(2,1)} fusion(f32[2,16,256,128]{3,2,1,0:T(8,128)} %param.13), kind=kLoop, calls=%fused_computation | loop fusion | flops 1048576 | bytes 6291456 | tf_op jit(solution)/shard_map/transpose | solution.py:325
  3.8 3.3 %copy.14 = bf16[2,128,16,256]{3,2,1,0:T(8,128)(2,1)S(1)} copy(bf16[2,128,16,256]{1,3,2,0:T(8,128)(2,1)} %convert_bitcast_fusion) | data formatting | bytes 4194304 | tf_op jit(solution)/shard_map/transpose | solution.py:325
  7.2 0.0 copy-start.3
  7.2 0.0 copy-start.6
  7.2 0.0 copy-start.8
  7.2 0.0 copy-start.9
  7.2 2.7 %convert_element_type.10 = bf16[1,4096,128]{2,1,0:T(8,128)(2,1)} convert(f32[1,4096,128]{2,1,0:T(8,128)} %param.12) | non-fusion elementwise | flops 524288 | bytes 3145728 | tf_op jit(solution)/shard_map/convert_element_type | solution.py:323
  9.9 1.9 %copy.13 = bf16[16,256,128]{1,0,2:T(8,128)(2,1)S(1)} copy(bf16[16,256,128]{2,1,0:T(8,128)(2,1)} %bitcast.14) | data formatting | bytes 2097152 | tf_op jit(solution)/shard_map/convert_element_type | solution.py:323
  11.8 0.0 copy-done.3
  11.8 0.0 copy-done.6
  11.8 0.0 copy-done.8
  11.8 0.0 copy-done.9
  11.8 0.0 copy-start
  11.8 1.0 %copy-done = bf16[512,512]{1,0:T(8,128)(2,1)S(1)} copy-done((bf16[512,512]{1,0:T(8,128)(2,1)S(1)}, bf16[512,512]{1,0:T(8,128)(2,1)}, u32[]{:S(2)}) %copy-start) | copy-done | bytes 524312
  12.9 0.0 copy-start.1
  12.9 1.0 %copy-done.1 = bf16[512,512]{1,0:T(8,128)(2,1)S(1)} copy-done((bf16[512,512]{1,0:T(8,128)(2,1)S(1)}, bf16[512,512]{1,0:T(8,128)(2,1)}, u32[]{:S(2)}) %copy-start.1) | copy-done | bytes 524312
  13.9 0.0 copy-start.2
  13.9 1.0 %copy-done.2 = f32[2,256,256]{2,1,0:T(8,128)S(1)} copy-done((f32[2,256,256]{2,1,0:T(8,128)S(1)}, f32[2,256,256]{2,1,0:T(8,128)}, u32[]{:S(2)}) %copy-start.2) | copy-done | bytes 524312
  15.0 0.0 copy-start.4
  15.0 0.9 %copy-done.4 = bf16[512,256]{1,0:T(8,128)(2,1)S(1)} copy-done((bf16[512,256]{1,0:T(8,128)(2,1)S(1)}, bf16[512,256]{1,0:T(8,128)(2,1)}, u32[]{:S(2)}) %copy-start.4) | copy-done | bytes 262168
  15.9 0.0 copy-start.5
  15.9 0.9 %copy-done.5 = bf16[256,512]{1,0:T(8,128)(2,1)S(1)} copy-done((bf16[256,512]{1,0:T(8,128)(2,1)S(1)}, bf16[256,512]{1,0:T(8,128)(2,1)}, u32[]{:S(2)}) %copy-start.5) | copy-done | bytes 262168
  16.9 0.0 copy-start.7
  16.9 0.9 copy-done.7
  17.8 72.7 %hyena.1 = bf16[8,512,128]{2,1,0:T(8,128)(2,1)S(1)} custom-call(bf16[4,4,2,4,16,256]{5,4,3,2,1,0:T(8,128)(2,1)S(1)} %bitcast.13, bf16[2,4,4,2,4,16,256]{6,5,4,3,2,1,0:T(8,128)(2,1)S(1)} %bitcast.11, bf16[128,1024]{1,0:T(8,128)(2,1)S(1)} %copy-done.3, s32[128]{0:T(128)S(1)} %copy-done.8, f32[128]{0:T(128)S(1)} %copy-done.9, bf16[512,256]{1,0:T(8,128)(2,1)S(1)} %copy-done.4, ...), custom_call_target="tpu_custom_call" | custom-call | tf_op jit(solution)/shard_map/hyena/pallas_call | solution.py:333
  90.5 1.5 %bitcast_convert_fusion = f32[1,4096,128]{2,1,0:T(8,128)} fusion(bf16[1,4096,128]{2,1,0:T(8,128)(2,1)S(1)} %bitcast.12), kind=kLoop, calls=%fused_computation.1 | loop fusion | flops 524288 | bytes 3145728 | tf_op jit(solution)/shard_map/reshape | solution.py:361
Async XLA Ops:
  7.2 4.6 %copy-start.3 = (bf16[128,1024]{1,0:T(8,128)(2,1)S(1)}, bf16[128,1024]{1,0:T(8,128)(2,1)}, u32[]{:S(2)}) copy-start(bf16[128,1024]{1,0:T(8,128)(2,1)} %w.1) | copy-start | bytes 786436
  7.2 4.6 %copy-start.6 = (bf16[256,256]{1,0:T(8,128)(2,1)S(1)}, bf16[256,256]{1,0:T(8,128)(2,1)}, u32[]{:S(2)}) copy-start(bf16[256,256]{1,0:T(8,128)(2,1)} %constant.18.clone.refs_4_) | copy-start | bytes 393220
  7.2 4.6 %copy-start.8 = (s32[128]{0:T(128)S(1)}, s32[128]{0:T(128)}, u32[]{:S(2)}) copy-start(s32[128]{0:T(128)} %mode.1) | copy-start | bytes 1540
  7.2 4.6 %copy-start.9 = (f32[128]{0:T(128)S(1)}, f32[128]{0:T(128)}, u32[]{:S(2)}) copy-start(f32[128]{0:T(128)} %gain.1) | copy-start | bytes 1540
  11.8 1.0 %copy-start = (bf16[512,512]{1,0:T(8,128)(2,1)S(1)}, bf16[512,512]{1,0:T(8,128)(2,1)}, u32[]{:S(2)}) copy-start(bf16[512,512]{1,0:T(8,128)(2,1)} %constant.15.clone.refs_1_) | copy-start | bytes 1572868
  12.9 1.0 %copy-start.1 = (bf16[512,512]{1,0:T(8,128)(2,1)S(1)}, bf16[512,512]{1,0:T(8,128)(2,1)}, u32[]{:S(2)}) copy-start(bf16[512,512]{1,0:T(8,128)(2,1)} %constant.16.clone.refs_2_) | copy-start | bytes 1572868
  13.9 1.0 %copy-start.2 = (f32[2,256,256]{2,1,0:T(8,128)S(1)}, f32[2,256,256]{2,1,0:T(8,128)}, u32[]{:S(2)}) copy-start(f32[2,256,256]{2,1,0:T(8,128)} %constant.20.clone.refs_6_) | copy-start | bytes 1572868
  15.0 0.9 %copy-start.4 = (bf16[512,256]{1,0:T(8,128)(2,1)S(1)}, bf16[512,256]{1,0:T(8,128)(2,1)}, u32[]{:S(2)}) copy-start(bf16[512,256]{1,0:T(8,128)(2,1)} %constant.14.clone.refs_0_) | copy-start | bytes 786436
  15.9 0.9 %copy-start.5 = (bf16[256,512]{1,0:T(8,128)(2,1)S(1)}, bf16[256,512]{1,0:T(8,128)(2,1)}, u32[]{:S(2)}) copy-start(bf16[256,512]{1,0:T(8,128)(2,1)} %constant.17.clone.refs_3_) | copy-start | bytes 786436
  16.9 0.9 copy-start.7

commit v4 on v3

--- a/solution.py
+++ b/solution.py
@@ -16,30 +16,16 @@
 MESH = pl.DeviceIdType.MESH
 
 
-def tables():
+PITCH = 24
+
+
+def table():
     counter = np.arange(256)
-    angle = (counter[:, None] * counter[None, :] % 256) * (2.0 * math.pi / 256)
-    c, s = np.cos(angle), np.sin(angle)
-    first = np.concatenate([c, -s], 0)
-    second = np.block([[c, -s], [s, c]])
-    third = np.block([[c, s], [-s, c]])
-    last = np.concatenate([c, -s], 1) / LENGTH
-    twist = counter[:, None] * counter[None, :] * (2.0 * math.pi / LENGTH)
-    twist = np.stack([np.cos(twist), np.sin(twist)])
-    scatter = np.zeros((256, 256))
-    for m in range(4):
-        for t in range(4):
-            for a in range(16):
-                x, k, a2 = a // 4, a // 2 % 2, a % 2
-                scatter[t * 64 + ((k * 4 + x) * 2 + a2) * 4 + m, (m * 4 + t) * 16 + a] = 1
-    regroup = np.zeros((256, 256))
-    for h in range(2):
-        for s in range(16):
-            for a2 in range(2):
-                for m in range(4):
-                    regroup[((h * 16 + s) * 2 + a2) * 4 + m, a2 * 128 + s * 8 + h * 4 + m] = 1
-    half = [jnp.asarray(t, BF16) for t in (first, second, third, last, scatter, regroup)]
-    return half + [jnp.asarray(twist, F32)]
+    product = counter[:, None] * counter[None, :]
+    angle = product % 256 * (2.0 * math.pi / 256)
+    twist = product * (2.0 * math.pi / LENGTH)
+    parts = [np.cos(angle), np.sin(angle), np.cos(twist), np.sin(twist)]
+    return jnp.asarray(np.stack(parts), F32)
 
 
 def flip(v, mask):
@@ -57,13 +43,13 @@
 
 
 def kernel(
-    sig, spec, w, mode, gain, *refs
+    signal, spectrum, w, mode, gain, table_hbm,
+    out,
+    raw, raw2, turned, sig, spec, twist,
+    first, second, third, last, scatter, regroup,
+    buf, final, spectral, hid, send, send1, gathered, gathered1, rows, wfull, prod,
+    h_sems, a_sems, b_sems, w_sems, d_sems, met,
 ):
-    tables_hbm, (
-        out, first, second, third, last, scatter, regroup, twist,
-        buf, final, spectral, hid, send, gathered, rows, wfull, prod,
-        t_sems, a_sems, b_sems, w_sems, d_sems, met,
-    ) = refs[:7], refs[7:]
     s = lax.axis_index("seq")
     c = lax.axis_index("ch")
     z, y, x, k = s // 4, lax.rem(s, 4), c // 2, lax.rem(c, 2)
@@ -95,14 +81,16 @@
                 if mask or core is other:
                     fn(flip(x, mask) * 2 + core)
 
-    copies = [
-        pltpu.make_async_copy(a, b, t_sems.at[i])
-        for i, (a, b) in enumerate(
-            zip(tables_hbm, (first, second, third, last, scatter, regroup, twist))
-        )
+    loads = [
+        pltpu.make_async_copy(signal.at[pl.ds(4 * i, 4)], raw.at[pl.ds(4 * i, 4)], h_sems.at[i])
+        for i in range(4)
     ]
-    for t in copies:
-        t.start()
+    loads += [
+        pltpu.make_async_copy(spectrum.at[i], raw2.at[i], h_sems.at[4 + i]) for i in range(2)
+    ]
+    loads.append(pltpu.make_async_copy(table_hbm, twist, h_sems.at[6]))
+    for load in loads:
+        load.start()
 
     barrier = pltpu.get_barrier_semaphore()
 
@@ -113,6 +101,31 @@
         greet(zdev(mask))
         greet(ydev(mask))
     peers(lambda t: greet({"seq": s, "ch": t}))
+
+    def turn(source, lo, n):
+        def step(a, carry):
+            value = source[a].T
+            turned.at[0][pl.ds(a, 128, stride=PITCH), :] = value[:, :128]
+            turned.at[1][pl.ds(a, 128, stride=PITCH), :] = value[:, 128:]
+            return carry
+
+        lax.fori_loop(lo, lo + n, step, 0)
+
+    def pack(target):
+        def step(t, carry):
+            for h in range(2):
+                for m in range(4):
+                    at = pl.ds(pl.multiple_of((t * 8 + h * 4 + m) * PITCH, 8), 16)
+                    value = jnp.concatenate([turned[0, at, :], turned[1, at, :]], 1)
+                    target[t // 4, lax.rem(t, 4), h, m] = value.astype(BF16)
+            return carry
+
+        lax.fori_loop(0, 16, step, 0)
+
+    for i in range(4):
+        loads[i].wait()
+        turn(raw, 4 * i, 4)
+    pack(sig)
     pl.semaphore_wait(barrier, 13)
 
     class Plane:
@@ -167,7 +180,7 @@
 
     def twists(ch):
         on = mode[s * 8 + ch] == 1
-        return jnp.where(on, twist[0], 1.0), jnp.where(on, twist[1], 0.0)
+        return jnp.where(on, twist[2], 1.0), jnp.where(on, twist[3], 0.0)
 
     def forward(h, lo):
         def step(m, carry):
@@ -200,25 +213,47 @@
 
         lax.fori_loop(lo, lo + 2, step, 0)
 
+    def build():
+        cos, sin = twist[0], twist[1]
+        first[:256], first[256:] = cos.astype(BF16), (-sin).astype(BF16)
+        second[:256, :256] = second[256:, 256:] = cos.astype(BF16)
+        third[:256, :256] = third[256:, 256:] = cos.astype(BF16)
+        second[:256, 256:] = third[256:, :256] = (-sin).astype(BF16)
+        second[256:, :256] = third[:256, 256:] = sin.astype(BF16)
+        last[:, :256] = (cos / LENGTH).astype(BF16)
+        last[:, 256:] = (-sin / LENGTH).astype(BF16)
+        i = lax.broadcasted_iota(jnp.int32, (256, 256), 0)
+        j = lax.broadcasted_iota(jnp.int32, (256, 256), 1)
+        m, t, at = j >> 6, (j >> 4) & 3, j & 15
+        row = t * 64 + ((at >> 1) & 1) * 32 + (at >> 2) * 8 + (at & 1) * 4 + m
+        scatter[...] = jnp.where(i == row, 1.0, 0.0).astype(BF16)
+        column = ((i >> 2) & 1) * 128 + ((i >> 3) & 15) * 8 + (i >> 7) * 4 + (i & 3)
+        regroup[...] = jnp.where(j == column, 1.0, 0.0).astype(BF16)
+
     def place(h):
         for t in range(4):
             block = hid[:, t].reshape(256, 256)
             value = dot(scatter[...], block).astype(BF16)
-            send[h, t * 32 : (t + 1) * 32] = value.reshape(32, 8, 256)
+            if h == 0:
+                send[t * 32 : (t + 1) * 32] = value.reshape(32, 8, 256)
+            else:
+                for e in range(2):
+                    part = value[:, e * 128 : (e + 1) * 128]
+                    send1[e, t * 32 : (t + 1) * 32] = part.reshape(32, 8, 128)
 
     sb, rb = b_sems
     mine = c * 16 + s
 
-    def scatter_all(h):
+    def scatter_all(source, target, i_sem):
         def step(i, carry):
             zz, yy = lax.rem(z + lax.rem(i, 4), 4), lax.rem(y + i // 4, 4)
             block = (zz * 4 + yy) * 8
             for mask in (2, 1, 3, 0):
                 for core in (k, other):
                     xx = flip(x, mask)
-                    part = send.at[h, block + core * 4 + xx]
+                    part = source.at[block + core * 4 + xx]
                     to = {"seq": zz * 4 + yy, "ch": xx * 2 + core}
-                    one = copy(part, gathered.at[h, mine], sb.at[h], rb.at[h], to)
+                    one = copy(part, target.at[mine], sb.at[i_sem], rb.at[i_sem], to)
                     if mask == 0 and core is k:
 
                         @pl.when(i > 0)
@@ -230,7 +265,7 @@
             return carry
 
         lax.fori_loop(0, 16, step, 0)
-        gathered[h, mine] = send[h, s * 8 + k * 4 + x]
+        target[mine] = source[s * 8 + k * 4 + x]
 
     own = pl.ds(pl.multiple_of(c * 128, 128), 128)
     ws, wr = w_sems
@@ -240,24 +275,27 @@
         method(u + 1, *m)
 
     pair(A.F, 0)
-    pair(A.F, 2)
     pair(A.S, 0, 0)
+    for i in range(2):
+        loads[4 + i].wait()
+        turn(raw2.at[i], 0, 16)
+        pack(spec.at[i])
+        A.F(2 + i)
+    pair(A.S, 0, 1)
+    pair(A.S, 0, 3)
     pair(A.S, 2, 0)
-    pair(A.F, 4)
     peers(lambda t: copy(w, wfull.at[own], ws, wr, {"seq": s, "ch": t}).start())
     wfull[own] = w[...]
-    pair(A.S, 0, 1)
-    pair(A.S, 0, 3)
     pair(A.S, 0, 2)
+    pair(A.F, 4)
+    loads[6].wait()
+    build()
     pair(A.S, 2, 1)
     pair(A.S, 2, 3)
     pair(A.S, 2, 2)
     pair(A.S, 4, 0)
     A.done(0)
-    for t in copies:
-        t.wait()
     forward(0, 0)
-    pair(A.S, 4, 1)
     forward(0, 2)
     A.done(1)
     peers(
@@ -265,6 +303,7 @@
             met, 1, device_id={"seq": s, "ch": t}, device_id_type=MESH
         )
     )
+    pair(A.S, 4, 1)
     forward(1, 0)
     pair(A.S, 4, 3)
     forward(1, 2)
@@ -275,89 +314,110 @@
     inverse(0, 2)
     place(0)
     pl.semaphore_wait(met, 7)
-    scatter_all(0)
+    scatter_all(send, gathered, 0)
     A.done(4)
     A.done(5)
     inverse(1, 0)
     inverse(1, 2)
     place(1)
-    scatter_all(1)
+    scatter_all(send1.at[0], gathered1.at[0], 1)
+    scatter_all(send1.at[1], gathered1.at[1], 2)
     recv(wfull.at[pl.ds(0, 7 * 128)], wr)
-    recv(gathered.at[0, pl.ds(0, 127)], rb.at[0])
-    recv(gathered.at[1, pl.ds(0, 127)], rb.at[1])
-
-    for i in range(8):
-        block = jnp.concatenate(
-            [gathered[h, 16 * i : 16 * i + 16].reshape(128, 256) for h in range(2)], 0
-        )
-        value = lax.dot_general(
-            block, regroup[...], (((0,), (0,)), ((), ())), preferred_element_type=F32
-        ).astype(BF16)
-        rows[0, :, i * 128 : (i + 1) * 128] = value[:, :128]
-        rows[1, :, i * 128 : (i + 1) * 128] = value[:, 128:]
-
-    for i in range(4):
-        value = dot(rows[...].reshape(512, 1024), wfull[:, i * 256 : (i + 1) * 256]).astype(BF16)
-        prod[0, i] = value[:, :128]
-        prod[1, i] = value[:, 128:]
+    recv(gathered.at[pl.ds(0, 127)], rb.at[0])
 
     ds, dr = d_sems
 
-    def give(t):
-        part = prod.at[lax.rem(t, 2), t // 2]
-        copy(part, out.at[c], ds, dr, {"seq": s, "ch": t}).start()
-
-    peers(give)
-    out[c] = prod[k, x]
-    recv(out.at[pl.ds(0, 7)], dr)
+    def project(e):
+        recv(gathered1.at[e, pl.ds(0, 127)], rb.at[1 + e])
+        for i in range(8):
+            old = gathered[16 * i : 16 * i + 16, :, e * 128 : (e + 1) * 128].reshape(128, 128)
+            new = gathered1[e, 16 * i : 16 * i + 16].reshape(128, 128)
+            value = lax.dot_general(
+                jnp.concatenate([old, new], 0),
+                regroup[...],
+                (((0,), (0,)), ((), ())),
+                preferred_element_type=F32,
+            ).astype(BF16)
+            rows[:128, i * 128 : (i + 1) * 128] = value[:, :128]
+            rows[128:, i * 128 : (i + 1) * 128] = value[:, 128:]
+        for mask in (2, 1, 3, 0):
+            xx = flip(x, mask)
+            columns = wfull[:, pl.ds(pl.multiple_of(xx * 256, 256), 256)]
+            value = dot(rows[...], columns).astype(BF16)
+            for core in range(2):
+                part = value[:, core * 128 : (core + 1) * 128]
+                prod[e, xx * 2 + core] = part.reshape(2, 128, 128)
+            for core in (k, other):
+                if mask or core is other:
+                    to = {"seq": s, "ch": xx * 2 + core}
+                    part = prod.at[e, xx * 2 + core]
+                    copy(part, out.at[c, :, e], ds.at[e], dr.at[e], to).start()
+        out[c, :, e] = prod[e, c]
+
+    project(0)
+    project(1)
+    for e in range(2):
+        recv(prod.at[e, pl.ds(0, 7)], dr.at[e])
 
     for u in range(6):
         A.drain(u)
-    for h in range(2):
-        sent(send.at[h, pl.ds(0, 127)], sb.at[h])
+    sent(send.at[pl.ds(0, 127)], sb.at[0])
+    for e in range(2):
+        sent(send1.at[e, pl.ds(0, 127)], sb.at[1 + e])
+        sent(prod.at[e, pl.ds(0, 7)], ds.at[e])
     sent(wfull.at[pl.ds(0, 7 * 128)], ws)
-    sent(out.at[pl.ds(0, 7)], ds)
 
 
 def per_device(signal, spectrum, channel_mode, skip_gain, out_weight):
-    pieces = signal.reshape(16, 256, 128).astype(BF16).transpose(2, 0, 1)
-    pieces = pieces.reshape(4, 4, 2, 4, 16, 256)
-    filters = spectrum.astype(BF16).transpose(0, 3, 1, 2)
-    filters = filters.reshape(2, 4, 4, 2, 4, 16, 256)
     unit = (4, 16, 256)
     dma = pltpu.SemaphoreType.DMA
-    constants = tables()
-    anywhere = pl.BlockSpec(memory_space=pltpu.HBM)
+    constant = table()
     vmem = pl.BlockSpec(memory_space=pltpu.VMEM)
     smem = pl.BlockSpec(memory_space=pltpu.SMEM)
+    hbm = pl.BlockSpec(memory_space=pltpu.HBM)
     result = pl.pallas_call(
         kernel,
-        out_shape=jax.ShapeDtypeStruct((8, 512, 128), BF16),
-        in_specs=[vmem, vmem, vmem, smem, smem] + [anywhere] * 7,
+        out_shape=jax.ShapeDtypeStruct((8, 2, 2, 128, 128), BF16),
+        in_specs=[hbm, hbm, vmem, smem, smem, hbm],
         out_specs=vmem,
         scratch_shapes=[
-            *(pltpu.VMEM(t.shape, t.dtype) for t in constants),
+            pltpu.VMEM((16, 256, 128), F32),
+            pltpu.VMEM((2, 16, 256, 128), F32),
+            pltpu.VMEM((2, 128 * PITCH, 128), F32),
+            pltpu.VMEM((4, 4, 2) + unit, BF16),
+            pltpu.VMEM((2, 4, 4, 2) + unit, BF16),
+            pltpu.VMEM((4, 256, 256), F32),
+            pltpu.VMEM((512, 256), BF16),
+            pltpu.VMEM((512, 512), BF16),
+            pltpu.VMEM((512, 512), BF16),
+            pltpu.VMEM((256, 512), BF16),
+            pltpu.VMEM((256, 256), BF16),
+            pltpu.VMEM((256, 256), BF16),
             pltpu.VMEM((6, 3, 4) + unit, BF16),
             pltpu.VMEM((6, 4, 4) + unit, BF16),
             pltpu.VMEM((8, 256, 512), F32),
             pltpu.VMEM((4, 4, 4, 16, 256), BF16),
-            pltpu.VMEM((2, 128, 8, 256), BF16),
-            pltpu.VMEM((2, 128, 8, 256), BF16),
-            pltpu.VMEM((2, 256, 1024), BF16),
+            pltpu.VMEM((128, 8, 256), BF16),
+            pltpu.VMEM((2, 128, 8, 128), BF16),
+            pltpu.VMEM((128, 8, 256), BF16),
+            pltpu.VMEM((2, 128, 8, 128), BF16),
+            pltpu.VMEM((256, 1024), BF16),
             pltpu.VMEM((1024, 1024), BF16),
-            pltpu.VMEM((2, 4, 512, 128), BF16),
+            pltpu.VMEM((2, 8, 2, 128, 128), BF16),
             dma((7,)),
             (dma((6,)), dma((6,)), dma((6,)), dma((6, 3))),
+            (dma((3,)), dma((3,))),
+            (dma, dma),
             (dma((2,)), dma((2,))),
-            (dma, dma),
-            (dma, dma),
             pltpu.SemaphoreType.REGULAR,
         ],
         compiler_params=pltpu.CompilerParams(
-            collective_id=0, has_side_effects=True, vmem_limit_bytes=40 << 20
+            collective_id=0, has_side_effects=True, vmem_limit_bytes=60 << 20
         ),
         name="hyena",
-    )(pieces, filters, out_weight, channel_mode, skip_gain, *constants)
+    )(
+        signal.reshape(16, 256, 128), spectrum, out_weight, channel_mode, skip_gain, constant
+    )
     return result.astype(F32).reshape(1, 4096, 128)
 
 

time: 93.4 us -> 78.8 us (0.84)
  local copies, waits for them, and re-layouts: 11.1 us -> 0 us
  other arithmetic: 7.99 us -> 2.68 us
  Pallas kernels: 72.7 us -> 75 us
    unnamed x20 -> x0, local copies, waits for them, and re-layouts: 5.95 us -> none
    transpose x1 -> x0, other arithmetic: 3.83 us -> none  [per_device(): filters = spectrum.astype(BF16).transpose(0, 3, 1, 2)]
    transpose x1 -> x0, local copies, waits for them, and re-layouts: 3.34 us -> none  [per_device(): filters = spectrum.astype(BF16).transpose(0, 3, 1, 2)]
    convert_element_type x1 -> x0, other arithmetic: 2.71 us -> none  [per_device(): pieces = signal.reshape(16, 256, 128).astype(BF16).transpose(2, 0, 1)]
    pallas_call x1, Pallas kernels: 72.7 us -> 75 us  [per_device(): pl.pallas_call(kernel, out_shape=jax.ShapeDtypeStruct((8, 2, 2, 128, 128)...]
    convert_element_type x1 -> x0, local copies, waits for them, and re-layouts: 1.86 us -> none  [per_device(): pieces = signal.reshape(16, 256, 128).astype(BF16).transpose(2, 0, 1)]
    reshape x1, other arithmetic: 1.46 us -> 2.68 us  [per_device(): return result.astype(F32).reshape(1, 4096, 128)]
where the time goes in v4:
time: 78.8 us; the launch traced here: 77.7 us
  Pallas kernels  75 us (95%)
  other arithmetic  2.68 us (3%)
    pallas_call x1, Pallas kernels, per_device(): pl.pallas_call(kernel, out_shape=jax.ShapeDtypeStruct((8, 2, 2, 128, 128)...  75 us
    reshape x1, other arithmetic, per_device(): return result.astype(F32).reshape(1, 4096, 128)  2.68 us

profile of v4, /device:TPU:0, one launch (start us, length us, event | category | flops | bytes accessed | tf_op | source)
XLA Modules:
  0.0 77.7 jit_solution(156009914282431417)
XLA Ops:
  0.0 75.0 %hyena.1 = bf16[8,2,2,128,128]{4,3,2,1,0:T(8,128)(2,1)} custom-call(f32[16,256,128]{2,1,0:T(8,128)} %bitcast.4, f32[2,16,256,128]{3,2,1,0:T(8,128)} %spectrum.1, bf16[128,1024]{1,0:T(8,128)(2,1)} %w.1, s32[128]{0:T(128)} %mode.1, f32[128]{0:T(128)} %gain.1, f32[4,256,256]{2,1,0:T(8,128)} %constant.2.clone.table_hbm), custom_call_target="tpu_custom_call" | custom-call | tf_op jit(solution)/shard_map/hyena/pallas_call | solution.py:378
  75.0 2.7 %convert.1 = f32[1,4096,128]{2,1,0:T(8,128)} convert(bf16[1,4096,128]{2,1,0:T(8,128)(2,1)} %bitcast.3) | non-fusion elementwise | flops 524288 | bytes 3145728 | tf_op jit(solution)/shard_map/reshape | solution.py:421

commit v5 on v4

--- a/solution.py
+++ b/solution.py
@@ -42,12 +42,16 @@
     return jnp.dot(a, b, preferred_element_type=F32)
 
 
+def flip2(v, step):
+    return lax.rem(v + jnp.where(step == 3, 2, jnp.where(step == 2, 3, step)), 4)
+
+
 def kernel(
-    signal, spectrum, w, mode, gain, table_hbm,
+    signal, spectrum, w_hbm, mode_hbm, gain_hbm, table_hbm,
     out,
-    raw, raw2, turned, sig, spec, twist,
-    first, second, third, last, scatter, regroup,
-    buf, final, spectral, hid, send, send1, gathered, gathered1, rows, wfull, prod,
+    raw, raw2, turned, sig, spec, twist, w, mode, gain,
+    first, second, third, last, scatter, regroup, order,
+    buf, final, spectral, hid, send, gathered, rows, total, wmine, wfull, prod,
     h_sems, a_sems, b_sems, w_sems, d_sems, met,
 ):
     s = lax.axis_index("seq")
@@ -88,7 +92,9 @@
     loads += [
         pltpu.make_async_copy(spectrum.at[i], raw2.at[i], h_sems.at[4 + i]) for i in range(2)
     ]
-    loads.append(pltpu.make_async_copy(table_hbm, twist, h_sems.at[6]))
+    small = ((table_hbm, twist), (w_hbm, w), (mode_hbm, mode), (gain_hbm, gain))
+    for i, (a, b) in enumerate(small):
+        loads.append(pltpu.make_async_copy(a, b, h_sems.at[6 + i]))
     for load in loads:
         load.start()
 
@@ -192,7 +198,7 @@
             spectral[4 * h + m] = dot(pair, second[...])
             return carry
 
-        lax.fori_loop(lo, lo + 2, step, 0)
+        lax.fori_loop(lo, lo + 2, step, 0, unroll=True)
 
     def inverse(h, lo):
         def step(m, carry):
@@ -211,7 +217,7 @@
             hid[m] = value.astype(BF16).reshape(4, 4, 16, 256)
             return carry
 
-        lax.fori_loop(lo, lo + 2, step, 0)
+        lax.fori_loop(lo, lo + 2, step, 0, unroll=True)
 
     def build():
         cos, sin = twist[0], twist[1]
@@ -227,33 +233,37 @@
         m, t, at = j >> 6, (j >> 4) & 3, j & 15
         row = t * 64 + ((at >> 1) & 1) * 32 + (at >> 2) * 8 + (at & 1) * 4 + m
         scatter[...] = jnp.where(i == row, 1.0, 0.0).astype(BF16)
-        column = ((i >> 2) & 1) * 128 + ((i >> 3) & 15) * 8 + (i >> 7) * 4 + (i & 3)
+        column = ((i >> 2) & 1) * 128 + (i >> 7) * 64 + ((i >> 3) & 15) * 4 + (i & 3)
         regroup[...] = jnp.where(j == column, 1.0, 0.0).astype(BF16)
+        i, j = i[:128, :128], j[:128, :128]
+        row = ((j >> 2) & 1) * 64 + (j >> 3) * 4 + (j & 3)
+        order[...] = jnp.where(i == row, 1.0, 0.0).astype(BF16)
 
     def place(h):
         for t in range(4):
             block = hid[:, t].reshape(256, 256)
             value = dot(scatter[...], block).astype(BF16)
-            if h == 0:
-                send[t * 32 : (t + 1) * 32] = value.reshape(32, 8, 256)
-            else:
-                for e in range(2):
-                    part = value[:, e * 128 : (e + 1) * 128]
-                    send1[e, t * 32 : (t + 1) * 32] = part.reshape(32, 8, 128)
+            for e in range(2):
+                part = value[:, e * 128 : (e + 1) * 128]
+                send[h, e, t * 32 : (t + 1) * 32] = part.reshape(32, 8, 128)
 
     sb, rb = b_sems
     mine = c * 16 + s
 
-    def scatter_all(source, target, i_sem):
+    def scatter_all(h, e):
+        source, target = send.at[h, e], gathered.at[h, e]
+        sem, done = sb.at[h, e], rb.at[h, e]
+
         def step(i, carry):
-            zz, yy = lax.rem(z + lax.rem(i, 4), 4), lax.rem(y + i // 4, 4)
+            i = 15 - i
+            zz, yy = flip2(z, lax.rem(i, 4)), flip2(y, i // 4)
             block = (zz * 4 + yy) * 8
             for mask in (2, 1, 3, 0):
                 for core in (k, other):
                     xx = flip(x, mask)
                     part = source.at[block + core * 4 + xx]
                     to = {"seq": zz * 4 + yy, "ch": xx * 2 + core}
-                    one = copy(part, target.at[mine], sb.at[i_sem], rb.at[i_sem], to)
+                    one = copy(part, target.at[mine], sem, done, to)
                     if mask == 0 and core is k:
 
                         @pl.when(i > 0)
@@ -267,7 +277,6 @@
         lax.fori_loop(0, 16, step, 0)
         target[mine] = source[s * 8 + k * 4 + x]
 
-    own = pl.ds(pl.multiple_of(c * 128, 128), 128)
     ws, wr = w_sems
 
     def pair(method, u, *m):
@@ -284,12 +293,14 @@
     pair(A.S, 0, 1)
     pair(A.S, 0, 3)
     pair(A.S, 2, 0)
-    peers(lambda t: copy(w, wfull.at[own], ws, wr, {"seq": s, "ch": t}).start())
-    wfull[own] = w[...]
+    for i in (6, 7, 8, 9):
+        loads[i].wait()
+    build()
+    wmine[...] = dot(order[...], w[...]).astype(BF16).reshape(2, 64, 1024)
+    peers(lambda t: copy(wmine, wfull.at[:, c], ws, wr, {"seq": s, "ch": t}).start())
+    wfull[:, c] = wmine[...]
     pair(A.S, 0, 2)
     pair(A.F, 4)
-    loads[6].wait()
-    build()
     pair(A.S, 2, 1)
     pair(A.S, 2, 3)
     pair(A.S, 2, 2)
@@ -314,36 +325,42 @@
     inverse(0, 2)
     place(0)
     pl.semaphore_wait(met, 7)
-    scatter_all(send, gathered, 0)
+    scatter_all(0, 0)
     A.done(4)
     A.done(5)
     inverse(1, 0)
     inverse(1, 2)
     place(1)
-    scatter_all(send1.at[0], gathered1.at[0], 1)
-    scatter_all(send1.at[1], gathered1.at[1], 2)
-    recv(wfull.at[pl.ds(0, 7 * 128)], wr)
-    recv(gathered.at[pl.ds(0, 127)], rb.at[0])
+    scatter_all(1, 0)
+    scatter_all(0, 1)
+    scatter_all(1, 1)
+    recv(wfull.at[:, pl.ds(0, 7)], wr)
 
     ds, dr = d_sems
 
-    def project(e):
-        recv(gathered1.at[e, pl.ds(0, 127)], rb.at[1 + e])
-        for i in range(8):
-            old = gathered[16 * i : 16 * i + 16, :, e * 128 : (e + 1) * 128].reshape(128, 128)
-            new = gathered1[e, 16 * i : 16 * i + 16].reshape(128, 128)
+    def arrange(h, e):
+        recv(gathered.at[h, e, pl.ds(0, 127)], rb.at[h, e])
+        for i in range(4):
             value = lax.dot_general(
-                jnp.concatenate([old, new], 0),
+                gathered[h, e, 32 * i : 32 * i + 32].reshape(256, 128),
                 regroup[...],
                 (((0,), (0,)), ((), ())),
                 preferred_element_type=F32,
             ).astype(BF16)
             rows[:128, i * 128 : (i + 1) * 128] = value[:, :128]
             rows[128:, i * 128 : (i + 1) * 128] = value[:, 128:]
+
+    def begin(e):
+        arrange(0, e)
+        total[...] = dot(rows[...], wfull[0].reshape(512, 1024))
+
+    def finish(e):
+        arrange(1, e)
         for mask in (2, 1, 3, 0):
             xx = flip(x, mask)
-            columns = wfull[:, pl.ds(pl.multiple_of(xx * 256, 256), 256)]
-            value = dot(rows[...], columns).astype(BF16)
+            columns = pl.ds(pl.multiple_of(xx * 256, 256), 256)
+            value = dot(rows[...], wfull[1, :, :, columns].reshape(512, 256))
+            value = (total[:, columns] + value).astype(BF16)
             for core in range(2):
                 part = value[:, core * 128 : (core + 1) * 128]
                 prod[e, xx * 2 + core] = part.reshape(2, 128, 128)
@@ -354,18 +371,20 @@
                     copy(part, out.at[c, :, e], ds.at[e], dr.at[e], to).start()
         out[c, :, e] = prod[e, c]
 
-    project(0)
-    project(1)
+    begin(0)
+    finish(0)
+    begin(1)
+    finish(1)
     for e in range(2):
         recv(prod.at[e, pl.ds(0, 7)], dr.at[e])
 
     for u in range(6):
         A.drain(u)
-    sent(send.at[pl.ds(0, 127)], sb.at[0])
     for e in range(2):
-        sent(send1.at[e, pl.ds(0, 127)], sb.at[1 + e])
+        for h in range(2):
+            sent(send.at[h, e, pl.ds(0, 127)], sb.at[h, e])
         sent(prod.at[e, pl.ds(0, 7)], ds.at[e])
-    sent(wfull.at[pl.ds(0, 7 * 128)], ws)
+    sent(wfull.at[:, pl.ds(0, 7)], ws)
 
 
 def per_device(signal, spectrum, channel_mode, skip_gain, out_weight):
@@ -373,12 +392,15 @@
     dma = pltpu.SemaphoreType.DMA
     constant = table()
     vmem = pl.BlockSpec(memory_space=pltpu.VMEM)
-    smem = pl.BlockSpec(memory_space=pltpu.SMEM)
     hbm = pl.BlockSpec(memory_space=pltpu.HBM)
+    fixed = [
+        pltpu.with_memory_space_constraint(t, pltpu.HBM)
+        for t in (out_weight, channel_mode, skip_gain)
+    ]
     result = pl.pallas_call(
         kernel,
         out_shape=jax.ShapeDtypeStruct((8, 2, 2, 128, 128), BF16),
-        in_specs=[hbm, hbm, vmem, smem, smem, hbm],
+        in_specs=[hbm] * 6,
         out_specs=vmem,
         scratch_shapes=[
             pltpu.VMEM((16, 256, 128), F32),
@@ -387,36 +409,40 @@
             pltpu.VMEM((4, 4, 2) + unit, BF16),
             pltpu.VMEM((2, 4, 4, 2) + unit, BF16),
             pltpu.VMEM((4, 256, 256), F32),
+            pltpu.VMEM((128, 1024), BF16),
+            pltpu.SMEM((128,), jnp.int32),
+            pltpu.SMEM((128,), F32),
             pltpu.VMEM((512, 256), BF16),
             pltpu.VMEM((512, 512), BF16),
             pltpu.VMEM((512, 512), BF16),
             pltpu.VMEM((256, 512), BF16),
             pltpu.VMEM((256, 256), BF16),
             pltpu.VMEM((256, 256), BF16),
+            pltpu.VMEM((128, 128), BF16),
             pltpu.VMEM((6, 3, 4) + unit, BF16),
             pltpu.VMEM((6, 4, 4) + unit, BF16),
             pltpu.VMEM((8, 256, 512), F32),
             pltpu.VMEM((4, 4, 4, 16, 256), BF16),
-            pltpu.VMEM((128, 8, 256), BF16),
-            pltpu.VMEM((2, 128, 8, 128), BF16),
-            pltpu.VMEM((128, 8, 256), BF16),
-            pltpu.VMEM((2, 128, 8, 128), BF16),
-            pltpu.VMEM((256, 1024), BF16),
-            pltpu.VMEM((1024, 1024), BF16),
+            pltpu.VMEM((2, 2, 128, 8, 128), BF16),
+            pltpu.VMEM((2, 2, 128, 8, 128), BF16),
+            pltpu.VMEM((256, 512), BF16),
+            pltpu.VMEM((256, 1024), F32),
+            pltpu.VMEM((2, 64, 1024), BF16),
+            pltpu.VMEM((2, 8, 64, 1024), BF16),
             pltpu.VMEM((2, 8, 2, 128, 128), BF16),
-            dma((7,)),
+            dma((10,)),
             (dma((6,)), dma((6,)), dma((6,)), dma((6, 3))),
-            (dma((3,)), dma((3,))),
+            (dma((2, 2)), dma((2, 2))),
             (dma, dma),
             (dma((2,)), dma((2,))),
             pltpu.SemaphoreType.REGULAR,
         ],
         compiler_params=pltpu.CompilerParams(
-            collective_id=0, has_side_effects=True, vmem_limit_bytes=60 << 20
+            collective_id=0, has_side_effects=True, vmem_limit_bytes=52 << 20
         ),
         name="hyena",
     )(
-        signal.reshape(16, 256, 128), spectrum, out_weight, channel_mode, skip_gain, constant
+        signal.reshape(16, 256, 128), spectrum, *fixed, constant
     )
     return result.astype(F32).reshape(1, 4096, 128)
 

time: 78.8 us -> 72.7 us (0.923)
  Pallas kernels: 75 us -> 70.2 us
  other arithmetic: 2.68 us -> 1.46 us
    pallas_call x1, Pallas kernels: 75 us -> 70.2 us  [per_device(): pl.pallas_call(kernel, out_shape=jax.ShapeDtypeStruct((8, 2, 2, 128, 128)...]
    reshape x1, other arithmetic: 2.68 us -> 1.46 us  [per_device(): return result.astype(F32).reshape(1, 4096, 128)]
where the time goes in v5:
time: 72.7 us; the launch traced here: 71.6 us
  Pallas kernels  70.2 us (97%)
  other arithmetic  1.46 us (2%)
    pallas_call x1, Pallas kernels, per_device(): pl.pallas_call(kernel, out_shape=jax.ShapeDtypeStruct((8, 2, 2, 128, 128)...  70.2 us
    reshape x1, other arithmetic, per_device(): return result.astype(F32).reshape(1, 4096, 128)  1.46 us

profile of v5, /device:TPU:0, one launch (start us, length us, event | category | flops | bytes accessed | tf_op | source)
XLA Modules:
  0.0 71.6 jit_solution(17238848290225862217)
XLA Ops:
  0.0 70.2 %hyena.1 = bf16[8,2,2,128,128]{4,3,2,1,0:T(8,128)(2,1)S(1)} custom-call(f32[16,256,128]{2,1,0:T(8,128)} %bitcast.4, f32[2,16,256,128]{3,2,1,0:T(8,128)} %spectrum.1, bf16[128,1024]{1,0:T(8,128)(2,1)} %w_hbm.1, s32[128]{0:T(128)} %mode_hbm.1, f32[128]{0:T(128)} %gain_hbm.1, f32[4,256,256]{2,1,0:T(8,128)} %constant.2.clone.table_hbm), custom_call_target="tpu_custom_call" | custom-call | tf_op jit(solution)/shard_map/hyena/pallas_call | solution.py:400
  70.2 1.5 %convert.1 = f32[1,4096,128]{2,1,0:T(8,128)} convert(bf16[1,4096,128]{2,1,0:T(8,128)(2,1)S(1)} %bitcast.3) | non-fusion elementwise | flops 524288 | bytes 3145728 | tf_op jit(solution)/shard_map/reshape | solution.py:447

commit v6 on v5

--- a/solution.py
+++ b/solution.py
@@ -115,7 +115,7 @@
             turned.at[1][pl.ds(a, 128, stride=PITCH), :] = value[:, 128:]
             return carry
 
-        lax.fori_loop(lo, lo + n, step, 0)
+        lax.fori_loop(lo, lo + n, step, 0, unroll=4)
 
     def pack(target):
         def step(t, carry):
@@ -250,32 +250,32 @@
     sb, rb = b_sems
     mine = c * 16 + s
 
-    def scatter_all(h, e):
+    def scatter_to(core, h, e):
         source, target = send.at[h, e], gathered.at[h, e]
         sem, done = sb.at[h, e], rb.at[h, e]
 
         def step(i, carry):
             i = 15 - i
             zz, yy = flip2(z, lax.rem(i, 4)), flip2(y, i // 4)
-            block = (zz * 4 + yy) * 8
+            block = (zz * 4 + yy) * 8 + core * 4
             for mask in (2, 1, 3, 0):
-                for core in (k, other):
-                    xx = flip(x, mask)
-                    part = source.at[block + core * 4 + xx]
-                    to = {"seq": zz * 4 + yy, "ch": xx * 2 + core}
-                    one = copy(part, target.at[mine], sem, done, to)
-                    if mask == 0 and core is k:
-
-                        @pl.when(i > 0)
-                        def _():
-                            one.start()
-
-                    else:
+                xx = flip(x, mask)
+                to = {"seq": zz * 4 + yy, "ch": xx * 2 + core}
+                one = copy(source.at[block + xx], target.at[mine], sem, done, to)
+                if mask:
+                    one.start()
+                else:
+
+                    @pl.when(jnp.logical_or(i > 0, k != core))
+                    def _():
                         one.start()
+
             return carry
 
         lax.fori_loop(0, 16, step, 0)
-        target[mine] = source[s * 8 + k * 4 + x]
+
+    def keep(h, e):
+        gathered[h, e, mine] = send[h, e, s * 8 + k * 4 + x]
 
     ws, wr = w_sems
 
@@ -290,6 +290,7 @@
         turn(raw2.at[i], 0, 16)
         pack(spec.at[i])
         A.F(2 + i)
+    pair(A.F, 4)
     pair(A.S, 0, 1)
     pair(A.S, 0, 3)
     pair(A.S, 2, 0)
@@ -300,40 +301,46 @@
     peers(lambda t: copy(wmine, wfull.at[:, c], ws, wr, {"seq": s, "ch": t}).start())
     wfull[:, c] = wmine[...]
     pair(A.S, 0, 2)
-    pair(A.F, 4)
+    pair(A.S, 4, 0)
     pair(A.S, 2, 1)
     pair(A.S, 2, 3)
     pair(A.S, 2, 2)
-    pair(A.S, 4, 0)
+    pair(A.S, 4, 1)
     A.done(0)
     forward(0, 0)
-    forward(0, 2)
+    pair(A.S, 4, 3)
     A.done(1)
     peers(
         lambda t: pl.semaphore_signal(
             met, 1, device_id={"seq": s, "ch": t}, device_id_type=MESH
         )
     )
-    pair(A.S, 4, 1)
+    forward(0, 2)
+    pair(A.S, 4, 2)
     forward(1, 0)
-    pair(A.S, 4, 3)
     forward(1, 2)
-    pair(A.S, 4, 2)
     A.done(2)
     A.done(3)
     inverse(0, 0)
     inverse(0, 2)
     place(0)
     pl.semaphore_wait(met, 7)
-    scatter_all(0, 0)
+    scatter_to(0, 0, 0)
     A.done(4)
     A.done(5)
+    scatter_to(1, 0, 0)
     inverse(1, 0)
     inverse(1, 2)
     place(1)
-    scatter_all(1, 0)
-    scatter_all(0, 1)
-    scatter_all(1, 1)
+    scatter_to(0, 1, 0)
+    scatter_to(0, 0, 1)
+    scatter_to(0, 1, 1)
+    scatter_to(1, 1, 0)
+    scatter_to(1, 0, 1)
+    scatter_to(1, 1, 1)
+    for e in range(2):
+        keep(0, e)
+        keep(1, e)
     recv(wfull.at[:, pl.ds(0, 7)], wr)
 
     ds, dr = d_sems

time: 72.7 us -> 69.5 us (0.956); the launches traced: 71.6 us -> 69.4 us
  Pallas kernels: 70.2 us -> 68 us
    pallas_call x1, Pallas kernels: 70.2 us -> 68 us  [per_device(): pl.pallas_call(kernel, out_shape=jax.ShapeDtypeStruct((8, 2, 2, 128, 128)...]
where the time goes in v6:
time: 69.5 us; the launch traced here: 69.4 us
  Pallas kernels  68 us (98%)
  other arithmetic  1.46 us (2%)
    pallas_call x1, Pallas kernels, per_device(): pl.pallas_call(kernel, out_shape=jax.ShapeDtypeStruct((8, 2, 2, 128, 128)...  68 us
    reshape x1, other arithmetic, per_device(): return result.astype(F32).reshape(1, 4096, 128)  1.46 us

profile of v6, /device:TPU:0, one launch (start us, length us, event | category | flops | bytes accessed | tf_op | source)
XLA Modules:
  0.0 69.4 jit_solution(6127649749283334468)
XLA Ops:
  0.0 68.0 %hyena.1 = bf16[8,2,2,128,128]{4,3,2,1,0:T(8,128)(2,1)S(1)} custom-call(f32[16,256,128]{2,1,0:T(8,128)} %bitcast.4, f32[2,16,256,128]{3,2,1,0:T(8,128)} %spectrum.1, bf16[128,1024]{1,0:T(8,128)(2,1)} %w_hbm.1, s32[128]{0:T(128)} %mode_hbm.1, f32[128]{0:T(128)} %gain_hbm.1, f32[4,256,256]{2,1,0:T(8,128)} %constant.2.clone.table_hbm), custom_call_target="tpu_custom_call" | custom-call | tf_op jit(solution)/shard_map/hyena/pallas_call | solution.py:407
  68.0 1.5 %convert.1 = f32[1,4096,128]{2,1,0:T(8,128)} convert(bf16[1,4096,128]{2,1,0:T(8,128)(2,1)S(1)} %bitcast.3) | non-fusion elementwise | flops 524288 | bytes 3145728 | tf_op jit(solution)/shard_map/reshape | solution.py:454

commit v7 on v6

--- a/solution.py
+++ b/solution.py
@@ -51,7 +51,7 @@
     out,
     raw, raw2, turned, sig, spec, twist, w, mode, gain,
     first, second, third, last, scatter, regroup, order,
-    buf, final, spectral, hid, send, gathered, rows, total, wmine, wfull, prod,
+    buf, final, spectral, mixed, hid, send, gathered, rows, total, wmine, wfull, prod,
     h_sems, a_sems, b_sems, w_sems, d_sems, met,
 ):
     s = lax.axis_index("seq")
@@ -184,9 +184,10 @@
 
     A = Plane(grab_inputs, buf, final, a_sems)
 
-    def twists(ch):
+    def twists(ch, columns=slice(None)):
         on = mode[s * 8 + ch] == 1
-        return jnp.where(on, twist[2], 1.0), jnp.where(on, twist[3], 0.0)
+        tc = jnp.where(on, twist[2, :, columns], 1.0)
+        return tc, jnp.where(on, twist[3, :, columns], 0.0)
 
     def forward(h, lo):
         def step(m, carry):
@@ -200,32 +201,47 @@
 
         lax.fori_loop(lo, lo + 2, step, 0, unroll=True)
 
-    def inverse(h, lo):
-        def step(m, carry):
-            value = spectral[4 * h + m]
-            re, im = value[:, :256], value[:, 256:]
-            fr = final[2 + 2 * h, :, :, m].reshape(256, 256).astype(F32)
-            fi = final[3 + 2 * h, :, :, m].reshape(256, 256).astype(F32)
-            pair = jnp.concatenate([re * fr - im * fi, re * fi + im * fr], 1).astype(BF16)
-            value = dot(pair, third[...])
-            re, im = value[:, :256], value[:, 256:]
-            tc, ts = twists(4 * h + m)
-            pair = jnp.concatenate([re * tc - im * ts, re * ts + im * tc], 0).astype(BF16)
-            value = dot(last[...], pair)
-            image = final[h, :, :, m].reshape(256, 256).astype(F32)
-            value = value + gain[s * 8 + 4 * h + m] * image
-            hid[m] = value.astype(BF16).reshape(4, 4, 16, 256)
+    def inverse(h, e):
+        columns = slice(e * 128, e * 128 + 128)
+
+        def step(j, carry):
+            parts = []
+            for m in (2 * j, 2 * j + 1):
+                if e == 0:
+                    value = spectral[4 * h + m]
+                    re, im = value[:, :256], value[:, 256:]
+                    fr = final[2 + 2 * h, :, :, m].reshape(256, 256).astype(F32)
+                    fi = final[3 + 2 * h, :, :, m].reshape(256, 256).astype(F32)
+                    pair = jnp.concatenate([re * fr - im * fi, re * fi + im * fr], 1).astype(BF16)
+                    mixed[m] = pair
+                else:
+                    pair = mixed[m]
+                value = dot(pair, third[e])
+                re, im = value[:, :128], value[:, 128:]
+                tc, ts = twists(4 * h + m, columns)
+                pair = jnp.concatenate([re * tc - im * ts, re * ts + im * tc], 0)
+                parts.append(pair.astype(BF16))
+            value = dot(last[...], jnp.concatenate(parts, 1))
+            for n in range(2):
+                m = 2 * j + n
+                image = final[h, :, :, m, :, columns].reshape(256, 128).astype(F32)
+                part = value[:, n * 128 : (n + 1) * 128] + gain[s * 8 + 4 * h + m] * image
+                hid[e, m] = part.astype(BF16).reshape(4, 4, 16, 128)
             return carry
 
-        lax.fori_loop(lo, lo + 2, step, 0, unroll=True)
+        lax.fori_loop(0, 2, step, 0, unroll=True)
 
     def build():
         cos, sin = twist[0], twist[1]
         first[:256], first[256:] = cos.astype(BF16), (-sin).astype(BF16)
         second[:256, :256] = second[256:, 256:] = cos.astype(BF16)
-        third[:256, :256] = third[256:, 256:] = cos.astype(BF16)
-        second[:256, 256:] = third[256:, :256] = (-sin).astype(BF16)
-        second[256:, :256] = third[:256, 256:] = sin.astype(BF16)
+        second[:256, 256:] = (-sin).astype(BF16)
+        second[256:, :256] = sin.astype(BF16)
+        for e in range(2):
+            part = slice(e * 128, e * 128 + 128)
+            third[e, :256, :128] = third[e, 256:, 128:] = cos[:, part].astype(BF16)
+            third[e, 256:, :128] = (-sin[:, part]).astype(BF16)
+            third[e, :256, 128:] = sin[:, part].astype(BF16)
         last[:, :256] = (cos / LENGTH).astype(BF16)
         last[:, 256:] = (-sin / LENGTH).astype(BF16)
         i = lax.broadcasted_iota(jnp.int32, (256, 256), 0)
@@ -239,13 +255,13 @@
         row = ((j >> 2) & 1) * 64 + (j >> 3) * 4 + (j & 3)
         order[...] = jnp.where(i == row, 1.0, 0.0).astype(BF16)
 
-    def place(h):
-        for t in range(4):
-            block = hid[:, t].reshape(256, 256)
-            value = dot(scatter[...], block).astype(BF16)
-            for e in range(2):
-                part = value[:, e * 128 : (e + 1) * 128]
-                send[h, e, t * 32 : (t + 1) * 32] = part.reshape(32, 8, 128)
+    def place(h, e):
+        for t in (0, 2):
+            blocks = [hid[e, :, t + n].reshape(256, 128) for n in range(2)]
+            value = dot(scatter[...], jnp.concatenate(blocks, 1)).astype(BF16)
+            for n in range(2):
+                part = value[:, n * 128 : (n + 1) * 128]
+                send[h, e, (t + n) * 32 : (t + n + 1) * 32] = part.reshape(32, 8, 128)
 
     sb, rb = b_sems
     mine = c * 16 + s
@@ -322,18 +338,20 @@
     A.done(2)
     A.done(3)
     inverse(0, 0)
-    inverse(0, 2)
-    place(0)
+    place(0, 0)
     pl.semaphore_wait(met, 7)
     scatter_to(0, 0, 0)
+    inverse(0, 1)
+    place(0, 1)
     A.done(4)
     A.done(5)
     scatter_to(1, 0, 0)
     inverse(1, 0)
-    inverse(1, 2)
-    place(1)
+    place(1, 0)
     scatter_to(0, 1, 0)
     scatter_to(0, 0, 1)
+    inverse(1, 1)
+    place(1, 1)
     scatter_to(0, 1, 1)
     scatter_to(1, 1, 0)
     scatter_to(1, 0, 1)
@@ -421,7 +439,7 @@
             pltpu.SMEM((128,), F32),
             pltpu.VMEM((512, 256), BF16),
             pltpu.VMEM((512, 512), BF16),
-            pltpu.VMEM((512, 512), BF16),
+            pltpu.VMEM((2, 512, 256), BF16),
             pltpu.VMEM((256, 512), BF16),
             pltpu.VMEM((256, 256), BF16),
             pltpu.VMEM((256, 256), BF16),
@@ -429,7 +447,8 @@
             pltpu.VMEM((6, 3, 4) + unit, BF16),
             pltpu.VMEM((6, 4, 4) + unit, BF16),
             pltpu.VMEM((8, 256, 512), F32),
-            pltpu.VMEM((4, 4, 4, 16, 256), BF16),
+            pltpu.VMEM((4, 256, 512), BF16),
+            pltpu.VMEM((2, 4, 4, 4, 16, 128), BF16),
             pltpu.VMEM((2, 2, 128, 8, 128), BF16),
             pltpu.VMEM((2, 2, 128, 8, 128), BF16),
             pltpu.VMEM((256, 512), BF16),

time: 69.5 us -> 68.9 us (level)
  no operation moved by 1% of the time
where the time goes in v7:
time: 68.9 us; the launch traced here: 68.8 us
  Pallas kernels  67.4 us (98%)
  other arithmetic  1.46 us (2%)
    pallas_call x1, Pallas kernels, per_device(): pl.pallas_call(kernel, out_shape=jax.ShapeDtypeStruct((8, 2, 2, 128, 128)...  67.4 us
    reshape x1, other arithmetic, per_device(): return result.astype(F32).reshape(1, 4096, 128)  1.46 us

profile of v7, /device:TPU:0, one launch (start us, length us, event | category | flops | bytes accessed | tf_op | source)
XLA Modules:
  0.0 68.8 jit_solution(2114415587060951103)
XLA Ops:
  0.0 67.4 %hyena.1 = bf16[8,2,2,128,128]{4,3,2,1,0:T(8,128)(2,1)S(1)} custom-call(f32[16,256,128]{2,1,0:T(8,128)} %bitcast.4, f32[2,16,256,128]{3,2,1,0:T(8,128)} %spectrum.1, bf16[128,1024]{1,0:T(8,128)(2,1)} %w_hbm.1, s32[128]{0:T(128)} %mode_hbm.1, f32[128]{0:T(128)} %gain_hbm.1, f32[4,256,256]{2,1,0:T(8,128)} %constant.2.clone.table_hbm), custom_call_target="tpu_custom_call" | custom-call | tf_op jit(solution)/shard_map/hyena/pallas_call | solution.py:425
  67.4 1.5 %convert.1 = f32[1,4096,128]{2,1,0:T(8,128)} convert(bf16[1,4096,128]{2,1,0:T(8,128)(2,1)S(1)} %bitcast.3) | non-fusion elementwise | flops 524288 | bytes 3145728 | tf_op jit(solution)/shard_map/reshape | solution.py:473

commit v8 on v7

--- a/solution.py
+++ b/solution.py
@@ -430,7 +430,7 @@
         scratch_shapes=[
             pltpu.VMEM((16, 256, 128), F32),
             pltpu.VMEM((2, 16, 256, 128), F32),
-            pltpu.VMEM((2, 128 * PITCH, 128), F32),
+            pltpu.VMEM((2, 129 * PITCH, 128), F32),
             pltpu.VMEM((4, 4, 2) + unit, BF16),
             pltpu.VMEM((2, 4, 4, 2) + unit, BF16),
             pltpu.VMEM((4, 256, 256), F32),

time: 68.9 us -> 68.9 us (level)
  no operation moved by 1% of the time
where the time goes in v8:
time: 68.9 us; the launch traced here: 68.8 us
  Pallas kernels  67.4 us (98%)
  other arithmetic  1.46 us (2%)
    pallas_call x1, Pallas kernels, per_device(): pl.pallas_call(kernel, out_shape=jax.ShapeDtypeStruct((8, 2, 2, 128, 128)...  67.4 us
    reshape x1, other arithmetic, per_device(): return result.astype(F32).reshape(1, 4096, 128)  1.46 us

profile of v8, /device:TPU:0, one launch (start us, length us, event | category | flops | bytes accessed | tf_op | source)
XLA Modules:
  0.0 68.8 jit_solution(14263482366918158728)
XLA Ops:
  0.0 67.4 %hyena.1 = bf16[8,2,2,128,128]{4,3,2,1,0:T(8,128)(2,1)S(1)} custom-call(f32[16,256,128]{2,1,0:T(8,128)} %bitcast.4, f32[2,16,256,128]{3,2,1,0:T(8,128)} %spectrum.1, bf16[128,1024]{1,0:T(8,128)(2,1)} %w_hbm.1, s32[128]{0:T(128)} %mode_hbm.1, f32[128]{0:T(128)} %gain_hbm.1, f32[4,256,256]{2,1,0:T(8,128)} %constant.2.clone.table_hbm), custom_call_target="tpu_custom_call" | custom-call | tf_op jit(solution)/shard_map/hyena/pallas_call | solution.py:425
  67.4 1.5 %convert.1 = f32[1,4096,128]{2,1,0:T(8,128)} convert(bf16[1,4096,128]{2,1,0:T(8,128)(2,1)S(1)} %bitcast.3) | non-fusion elementwise | flops 524288 | bytes 3145728 | tf_op jit(solution)/shard_map/reshape | solution.py:473

commit v9 on v8

--- a/solution.py
+++ b/solution.py
@@ -86,16 +86,16 @@
                     fn(flip(x, mask) * 2 + core)
 
     loads = [
-        pltpu.make_async_copy(signal.at[pl.ds(4 * i, 4)], raw.at[pl.ds(4 * i, 4)], h_sems.at[i])
-        for i in range(4)
+        pltpu.make_async_copy(signal.at[pl.ds(2 * i, 2)], raw.at[pl.ds(2 * i, 2)], h_sems.at[i])
+        for i in range(8)
     ]
     loads += [
-        pltpu.make_async_copy(spectrum.at[i], raw2.at[i], h_sems.at[4 + i]) for i in range(2)
+        pltpu.make_async_copy(spectrum.at[i], raw2.at[i], h_sems.at[8 + i]) for i in range(2)
     ]
     small = ((table_hbm, twist), (w_hbm, w), (mode_hbm, mode), (gain_hbm, gain))
     for i, (a, b) in enumerate(small):
-        loads.append(pltpu.make_async_copy(a, b, h_sems.at[6 + i]))
-    for load in loads:
+        loads.append(pltpu.make_async_copy(a, b, h_sems.at[10 + i]))
+    for load in loads[:8]:
         load.start()
 
     barrier = pltpu.get_barrier_semaphore()
@@ -115,7 +115,7 @@
             turned.at[1][pl.ds(a, 128, stride=PITCH), :] = value[:, 128:]
             return carry
 
-        lax.fori_loop(lo, lo + n, step, 0, unroll=4)
+        lax.fori_loop(lo, lo + n, step, 0, unroll=min(n, 4))
 
     def pack(target):
         def step(t, carry):
@@ -128,9 +128,12 @@
 
         lax.fori_loop(0, 16, step, 0)
 
-    for i in range(4):
+    for i in range(8):
         loads[i].wait()
-        turn(raw, 4 * i, 4)
+        if i == 0:
+            for load in loads[8:]:
+                load.start()
+        turn(raw, 2 * i, 2)
     pack(sig)
     pl.semaphore_wait(barrier, 13)
 
@@ -302,7 +305,7 @@
     pair(A.F, 0)
     pair(A.S, 0, 0)
     for i in range(2):
-        loads[4 + i].wait()
+        loads[8 + i].wait()
         turn(raw2.at[i], 0, 16)
         pack(spec.at[i])
         A.F(2 + i)
@@ -310,8 +313,8 @@
     pair(A.S, 0, 1)
     pair(A.S, 0, 3)
     pair(A.S, 2, 0)
-    for i in (6, 7, 8, 9):
-        loads[i].wait()
+    for load in loads[10:]:
+        load.wait()
     build()
     wmine[...] = dot(order[...], w[...]).astype(BF16).reshape(2, 64, 1024)
     peers(lambda t: copy(wmine, wfull.at[:, c], ws, wr, {"seq": s, "ch": t}).start())
@@ -456,7 +459,7 @@
             pltpu.VMEM((2, 64, 1024), BF16),
             pltpu.VMEM((2, 8, 64, 1024), BF16),
             pltpu.VMEM((2, 8, 2, 128, 128), BF16),
-            dma((10,)),
+            dma((14,)),
             (dma((6,)), dma((6,)), dma((6,)), dma((6, 3))),
             (dma((2, 2)), dma((2, 2))),
             (dma, dma),

time: 68.9 us -> 69 us (level)
  no operation moved by 1% of the time
where the time goes in v9:
time: 69 us; the launch traced here: 68.8 us
  Pallas kernels  67.4 us (98%)
  other arithmetic  1.46 us (2%)
    pallas_call x1, Pallas kernels, per_device(): pl.pallas_call(kernel, out_shape=jax.ShapeDtypeStruct((8, 2, 2, 128, 128)...  67.4 us
    reshape x1, other arithmetic, per_device(): return result.astype(F32).reshape(1, 4096, 128)  1.46 us

profile of v9, /device:TPU:0, one launch (start us, length us, event | category | flops | bytes accessed | tf_op | source)
XLA Modules:
  0.0 68.8 jit_solution(6607150285145834073)
XLA Ops:
  0.0 67.4 %hyena.1 = bf16[8,2,2,128,128]{4,3,2,1,0:T(8,128)(2,1)S(1)} custom-call(f32[16,256,128]{2,1,0:T(8,128)} %bitcast.4, f32[2,16,256,128]{3,2,1,0:T(8,128)} %spectrum.1, bf16[128,1024]{1,0:T(8,128)(2,1)} %w_hbm.1, s32[128]{0:T(128)} %mode_hbm.1, f32[128]{0:T(128)} %gain_hbm.1, f32[4,256,256]{2,1,0:T(8,128)} %constant.2.clone.table_hbm), custom_call_target="tpu_custom_call" | custom-call | tf_op jit(solution)/shard_map/hyena/pallas_call | solution.py:428
  67.4 1.5 %convert.1 = f32[1,4096,128]{2,1,0:T(8,128)} convert(bf16[1,4096,128]{2,1,0:T(8,128)(2,1)S(1)} %bitcast.3) | non-fusion elementwise | flops 524288 | bytes 3145728 | tf_op jit(solution)/shard_map/reshape | solution.py:476
